TPU v7x, 512 devices: a 4x2x32 block of a 4x16x32 slice. The times are simulated.
512 devices in a mesh: parts: 2 (over y), tm: 32 (over z), sub: 4 (over x), inner: 2 (over core).
Axes of the slice: x: 4, y: 2, z: 32, core: 2. Of those that a mesh axis runs over, the one named last changes fastest.
The devices are a block of a 4x16x32 slice.
Arguments:
- guess: float32 [8192, 128], P(('parts', 'tm', 'sub', 'inner')), parts along dimension 0, may hold values from -6 to 6
- start: float32 [256], P('parts'), parts along dimension 0, may hold values from -6 to 6
- layer_weight: float32 [256, 64], replicated, may hold values from -0.75 to 0.75
- layer_bias: float32 [256], replicated, may hold values from -4 to 4
- amplitude: float32 [256], replicated, may hold values from 0.5 to 4
Outputs:
- updated: float32 [8192, 128], P(('parts', 'tm', 'sub', 'inner')), parts along dimension 0
There are 2 independent parts, one for each index of `parts`. A program takes and returns all parts, laid end to end along the dimension named above; an argument that names none is the same for every part. Nothing has to cross between parts.
All inputs are finite; a program needn't handle non-finite values.
Results may differ from a plain program's by a relative error of at most 0.0003.
Values sent between devices are 32-bit elements; how exact they have to be, the bound alone decides.
A program may use at most 128 MiB of HBM per device.

v0:
```python
import jax
import jax.numpy as jnp
from jax import lax
from jax.sharding import PartitionSpec as P

step_size = 0.04
curvature = 0.5


def from_behind(value, axis, steps):
    count = lax.axis_size(axis)
    first, last = (max(0, -steps), min(count, count - steps))
    return lax.ppermute(value, axis, [(source, source + steps) for source in range(first, last)])


def gathered_once(shard, axis):
    leaves = jax.tree.leaves(shard)
    turns = sorted(range(len(leaves)), key=lambda k: -leaves[k].size)
    width = (1, *leaves[turns[0]].shape)[-1]
    lines = [
        jnp.pad(leaves[k].reshape(-1), (0, -leaves[k].size % width)).reshape(-1, width)
        for k in turns
    ]
    both, at, found = (lax.all_gather(jnp.concatenate(lines), axis), 0, {})
    for k, line in zip(turns, lines):
        slab = both[:, at : at + len(line)].reshape(len(both), -1)
        found[k] = slab[:, : leaves[k].size].reshape(-1, *leaves[k].shape)
        at += len(line)
    numbers = iter(range(len(leaves)))
    return jax.tree.map(lambda _: found[next(numbers)], shard)


def prefix_2(value, axis, join, neutral):
    count, mine = (lax.axis_size(axis), lax.axis_index(axis))
    pieces = gathered_once(value, axis)
    running = jax.tree.map(
        lambda part, zero: jnp.full_like(part, 0) + jnp.asarray(zero, part.dtype), value, neutral
    )

    def turn(position, running):
        longer = join(running, jax.tree.map(lambda part: part[position], pieces))
        return jax.tree.map(lambda new, old: jnp.where(position < mine, new, old), longer, running)

    return lax.fori_loop(0, count - 1, turn, running)


def from_root(shard, axis, root):
    return lax.dynamic_index_in_dim(lax.all_gather(shard, axis), root, 0, keepdims=False)


def once_a_type(shard, axis):
    leaves, found = (jax.tree.leaves(shard), {})
    for first, a in enumerate(leaves):
        if first not in found:
            alike = [k for k, b in enumerate(leaves) if b.dtype == a.dtype]
            got = (
                gathered_once([leaves[k] for k in alike], axis)
                if len(alike) > 1
                else [lax.all_gather(a, axis)]
            )
            for k, b in zip(alike, got):
                found[k] = b
    numbers = iter(range(len(leaves)))
    return jax.tree.map(lambda _: found[next(numbers)], shard)


def carried_in(part, axis, combine, identity):
    place = lax.axis_index(axis)
    gathered = once_a_type(part, axis)
    state = jax.tree.map(lambda a, e: jnp.zeros_like(a) + jnp.asarray(e, a.dtype), part, identity)

    def one(turn, state):
        return combine(
            state, jax.tree.map(lambda a: lax.dynamic_index_in_dim(a, turn, 0, False), gathered)
        )

    return lax.fori_loop(0, place, one, state)


def forces(coords, layer_weight, layer_bias, amplitude):
    hi = lax.Precision.HIGHEST
    pre = jnp.dot(coords, layer_weight.T, precision=hi) + layer_bias
    gate = jax.nn.sigmoid(pre)
    grad = jnp.dot(amplitude * gate, layer_weight, precision=hi) + curvature * coords
    return (grad, amplitude * gate * (1.0 - gate))


def hess_apply(vector, layer_weight, weights_d):
    hi = lax.Precision.HIGHEST
    inner_vals = jnp.dot(layer_weight, vector, precision=hi) * weights_d
    return jnp.dot(inner_vals, layer_weight, precision=hi) + curvature * vector


def hessian(layer_weight, weights_d):
    hi = lax.Precision.HIGHEST
    width = layer_weight.shape[1]
    scaled = layer_weight * weights_d[:, None]
    return jnp.dot(scaled.T, layer_weight, precision=hi) + curvature * jnp.eye(
        width, dtype=jnp.float32
    )


def combine(earlier, later):
    hi = lax.Precision.HIGHEST
    map_early, shift_early = earlier
    map_late, shift_late = later
    return (
        jnp.dot(map_late, map_early, precision=hi),
        jnp.dot(map_late, shift_early, precision=hi) + shift_late,
    )


def shards(guess, start, layer_weight, layer_bias, amplitude):
    hi = lax.Precision.HIGHEST
    width = layer_weight.shape[1]
    state_len = 2 * width
    received = from_behind(guess[-1], ("tm", "sub", "inner"), 1)
    previous = jnp.where(lax.axis_index(("tm", "sub", "inner")) == 0, start, received)
    before = jnp.concatenate([previous[None, :], guess[:-1]], axis=0)
    coords, momenta = (before[:, :width], before[:, width:])
    grad_zero, curve_zero = forces(coords, layer_weight, layer_bias, amplitude)
    half = momenta - 0.5 * step_size * grad_zero
    moved = coords + step_size * half
    grad_one, curve_one = forces(moved, layer_weight, layer_bias, amplitude)
    landed = half - 0.5 * step_size * grad_one
    image = jnp.concatenate([moved, landed], axis=1)
    unit = jnp.eye(width, dtype=jnp.float32)

    def compose(carry, items):
        window_map, window_shift = carry
        prior, curve_a, curve_b, target = items
        hess_a = hessian(layer_weight, curve_a)
        hess_b = hessian(layer_weight, curve_b)
        block_qq = unit - 0.5 * step_size * step_size * hess_a
        block_pq = -0.5 * step_size * (hess_a + jnp.dot(hess_b, block_qq, precision=hi))
        block_pp = unit - 0.5 * step_size * step_size * hess_b
        jacobian = jnp.block([[block_qq, step_size * unit], [block_pq, block_pp]])
        offset = target - jnp.dot(jacobian, prior, precision=hi)
        new_map = jnp.dot(jacobian, window_map, precision=hi)
        new_shift = jnp.dot(jacobian, window_shift, precision=hi) + offset
        return ((new_map, new_shift), None)

    identity = (jnp.eye(state_len, dtype=jnp.float32), jnp.zeros((state_len,), jnp.float32))
    local, unused = lax.scan(compose, identity, (before, curve_zero, curve_one, image))
    lower = prefix_2(local, ("sub", "inner"), combine, identity)
    closing = combine(lower, local)
    total = (
        from_root(closing[0], ("sub", "inner"), lax.axis_size(("sub", "inner")) - 1),
        from_root(closing[1], ("sub", "inner"), lax.axis_size(("sub", "inner")) - 1),
    )
    major = carried_in(total, "tm", combine, identity)
    prefix = combine(major, lower)
    entering = jnp.dot(prefix[0], start, precision=hi) + prefix[1]

    def advance(state, items):
        prior, curve_a, curve_b, target = items
        delta = state - prior
        delta_q, delta_p = (delta[:width], delta[width:])
        first = hess_apply(delta_q, layer_weight, curve_a)
        new_q = delta_q - 0.5 * step_size * step_size * first + step_size * delta_p
        new_p = (
            delta_p
            - 0.5 * step_size * first
            - 0.5 * step_size * hess_apply(new_q, layer_weight, curve_b)
        )
        result = target + jnp.concatenate([new_q, new_p])
        return (result, result)

    final, states = lax.scan(advance, entering, (before, curve_zero, curve_one, image))
    return states


def solution(mesh):
    placed = (P(("parts", "tm", "sub", "inner"), None), P("parts"), P(), P(), P())
    return jax.shard_map(
        shards,
        mesh=mesh,
        in_specs=placed,
        out_specs=P(("parts", "tm", "sub", "inner"), None),
        check_vma=False,
    )
```

profile of v0, /device:TPU:34, one launch (start us, length us, event | category | flops | bytes accessed | tf_op | source)
XLA Modules:
  0.0 316.2 jit_solution(17509226477312185742)
XLA Ops:
  7.2 1.9 collective-permute-start
  9.3 2.9 collective-permute-done
  17.0 53.6 %while.57 = (s32[]{:T(128)}, f32[128,128]{1,0:T(8,128)S(1)}, f32[128]{0:T(128)S(1)}, f32[16,256]{1,0:T(8,128)S(1)}, f32[256,64]{0,1:T(8,128)}, /*index=5*/f32[16...) while((s32[]{:T(128)}, f32[128,128]{1,0:T(8,128)S(1)}, ...), condition=%wide.region_1.2_spmd.clone.clone, body=%wide.region_0.1_spmd.clone.clone.sunk | while | flops 54133120 | bytes 797811 | solution.py:144
  70.7 48.4 %all-gather.4 = f32[8,129,128]{2,1,0:T(8,128)S(1)} all-gather(f32[1,129,128]{2,1,0:T(8,128)S(1)} %maximum_bitcast_fusion), channel_id=2, replica_groups=mesh['parts'=2,'tm'=32,'sub'=4,'inner'=2] {'sub','inner'}, dimensions={0}, use_global_device_ids=true | all-gather | bytes 594432 | tf_op jit(solution)/shard_map/all_gather | solution.py:24
  119.2 3.4 %while.56 = (s32[]{:T(128)}, f32[128,128]{1,0:T(8,128)S(1)}, f32[128]{0:T(128)S(1)}, s32[]{:T(128)}, f32[8,128,128]{2,1,0:T(8,128)S(1)}, /*index=5*/f32[8,128]{1,0:T(8,128)S(1)}, s32[]{:T(128)}, s32[]{:T(128)}) while((s32[]{:T(128)}, f32[128,128]{1,0:T(8,128)S(1)}, f32[128]{0:T(128)S(1)}, s32[]{:T(128)}, ...), condition=%wide.region_3.4_spmd.clone, body=%wide.region_2.3_spmd.clone.sunk | while | flops 25379332 | bytes 464492 | solution.py:44
  122.8 13.3 %all-gather.1 = f32[1024,128]{1,0:T(8,128)S(1)} all-gather(f32[128,128]{1,0:T(8,128)S(1)} %fusion.80), channel_id=3, replica_groups=mesh['parts'=2,'tm'=32,'sub'=4,'inner'=2] {'sub','inner'}, dimensions={0}, use_global_device_ids=true | all-gather | bytes 589824 | tf_op jit(solution)/shard_map/all_gather | solution.py:48
  136.4 10.8 %all-gather.5 = f32[8,1,128]{2,1,0:T(1,128)S(1)} all-gather(f32[1,1,128]{2,1,0:T(1,128)S(1)} %fusion.64), channel_id=4, replica_groups=mesh['parts'=2,'tm'=32,'sub'=4,'inner'=2] {'sub','inner'}, dimensions={0}, use_global_device_ids=true | all-gather | bytes 4608 | tf_op jit(solution)/shard_map/all_gather | solution.py:48
  147.8 123.9 %all-gather.9.cloned.1.call-done = f32[32,129,128]{2,1,0:T(8,128)} async-done(((f32[1,129,128]{2,1,0:T(8,128)}), f32[32,129,128]{2,1,0:T(8,128)}) %all-gather.9.cloned.1.call-update) | async-done | bytes 2113552 | tf_op jit(solution)/shard_map/all_gather | solution.py:24
  271.7 1.7 slice.51
  275.1 34.3 %while.55 = (s32[]{:T(128)}, f32[128]{0:T(128)S(1)}, f32[16,128]{1,0:T(8,128)}, f32[16,128]{1,0:T(8,128)S(1)}, f32[16,128]{1,0:T(8,128)S(1)}, /*index=5*/f32[256...) while((s32[]{:T(128)}, f32[128]{0:T(128)S(1)}, ...), condition=%wide.region_7.8_spmd, body=%wide.region_6.7_spmd.sunk | while | flops 788354 | bytes 285049 | solution.py:169
  275.9 1.3 dynamic_update_slice.5
  278.0 1.3 dynamic_update_slice.5
  280.2 1.3 dynamic_update_slice.5
  282.3 1.3 dynamic_update_slice.5
  284.5 1.3 dynamic_update_slice.5
  286.6 1.3 dynamic_update_slice.5
  288.7 1.3 dynamic_update_slice.5
  290.9 1.3 dynamic_update_slice.5
  293.0 1.3 dynamic_update_slice.5
  295.1 1.3 dynamic_update_slice.5
  297.3 1.3 dynamic_update_slice.5
  299.4 1.3 dynamic_update_slice.5
  301.6 1.3 dynamic_update_slice.5
  303.7 1.3 dynamic_update_slice.5
  (383 shorter events, 79.7 us)
Async XLA Ops:
  6.5 265.2 %all-gather.9.cloned.1.call-start = ((), (), s32[]{:S(2)}) async-start(), calls=%async_computation | async-start | bytes 2297856 | tf_op jit(solution)/shard_map/all_gather | solution.py:24
  7.2 4.9 %collective-permute-start = (f32[128]{0:T(128)S(1)}, f32[128]{0:T(128)S(1)}, u32[]{:S(2)}, u32[]{:S(2)}) collective-permute-start(f32[128]{0:T(128)S(1)} %slice_bitcast_fusion.1), channel_id=1, source_target_pairs={{0,1},{1,2},{2,3},{3,4},{4,5},{5,6},{6,7},{7,8},{8,9},{9,10},{10,1... | collective-permute-start | bytes 1544 | tf_op jit(solution)/shard_map/ppermute | solution.py:13
  273.5 1.4 copy-start.1
  273.5 1.6 copy-start
Sparse Core Ops, SparseCore 0:
  147.9 123.7 all-gather.8
where the time goes:
time: 319 us; the launch traced here: 316 us
  waiting for transfers between devices  127 us (40%)
  blocking collectives  72.5 us (23%)
  matrix products  69 us (22%)
  local copies, waits for them, and re-layouts  25.7 us (8%)
  between operations  13.6 us (4%)
  other arithmetic  4.81 us (2%)
    all_gather x1, waiting for transfers between devices, gathered_once(): both, at, found = (lax.all_gather(jnp.concatenate(lines), axis), 0, {})  124 us
    all_gather x1, blocking collectives, gathered_once(): both, at, found = (lax.all_gather(jnp.concatenate(lines), axis), 0, {})  48.4 us
    dot_general x32, matrix products, hessian(): jnp.dot(scaled.T, layer_weight, precision=hi)  35.9 us
    all_gather x2, blocking collectives, from_root(): lax.all_gather(shard, axis)  24.1 us
    dynamic_update_slice x16, local copies, waits for them, and re-layouts, shards(): lax.scan(advance, entering, (before, curve_zero, curve_one, image))  20.8 us
  transfers between devices with their start and end apart: 2, of which 2 were waited for; matrix products, arithmetic and copies ran while one was open for 0% of the time, Pallas kernels for 0%

commit v1 on v0

v1 whole, which is shorter than its diff:
```python
import functools

import jax
import jax.numpy as jnp
from jax import lax
from jax.experimental import pallas as pl
from jax.experimental.pallas import tpu as pltpu
from jax.sharding import PartitionSpec as P

step_size = 0.04
curvature = 0.5
half_step = 0.5 * step_size
f32, bf16 = jnp.float32, jnp.bfloat16
MESH = pl.DeviceIdType.MESH
planes = 4
tail = 8


def iota(shape, axis):
    return lax.broadcasted_iota(jnp.int32, shape, axis)


def split(value):
    high = value.astype(bf16)
    return high, (value - high.astype(f32)).astype(bf16)


def low_lanes(value):
    width = value.shape[-1]
    return iota(value.shape, 1) < width // 2


def mixed(value):
    high = value.astype(bf16).astype(f32)
    return jnp.where(low_lanes(value), high, value - high).astype(bf16)


def twice(value):
    swapped = pltpu.roll(value, value.shape[-1] // 2, 1)
    low = low_lanes(value)
    return jnp.where(low, value, swapped), jnp.where(low, swapped, value)


def join(coords, momenta):
    return jnp.where(low_lanes(coords), coords, momenta)


def dot(left, right):
    return jnp.dot(left, right, preferred_element_type=f32)


def with_tail(value, extra):
    rows = value.shape[0] - tail
    return jnp.concatenate([value[:rows], value[rows:] + extra], axis=0)


def compose(first, second):
    state = first.shape[1]
    eye = (iota((state, state), 0) == iota((state, state), 1)).astype(f32)
    high, low = split(second[:state] - eye)
    both = jnp.concatenate([high, low], axis=1)
    left = jnp.concatenate(split(first), axis=1)
    out = dot(left, jnp.concatenate([both, both], axis=0))
    return with_tail(first + (out[:, :state] + out[:, state:]), second[state:])


def chain(maps):
    while len(maps) > 1:
        maps = [
            compose(maps[k], maps[k + 1]) if k + 1 < len(maps) else maps[k]
            for k in range(0, len(maps), 2)
        ]
    return maps[0]


def identity(state):
    rows = state + tail
    return (iota((rows, state), 0) == iota((rows, state), 1)).astype(f32)


def applied(vector, full):
    state = vector.shape[1]
    eye = iota((state, state), 0) == iota((state, state), 1)
    column = jnp.sum(jnp.where(eye, vector, 0.0), axis=1, keepdims=True)
    return jnp.sum(column * full[:state], axis=0, keepdims=True) + full[state : state + 1]


class Local:
    def __init__(self, guess, start, weight, bias, amplitude):
        self.steps, self.state = guess.shape
        steps = self.steps
        doubled = jnp.concatenate([weight, weight], axis=1)
        self.across = doubled.T
        high, low = split(self.across)
        self.onto = jnp.concatenate([high, low], axis=0)
        high, low = split(doubled)
        self.back = jnp.concatenate([high, low], axis=1)
        self.width = self.state // 2
        rows = jnp.concatenate([guess, jnp.broadcast_to(start, (tail, self.state))], axis=0)
        coords, momenta = twice(rows)
        grad_zero, curve_zero = self.forces(coords, bias, amplitude)
        half = momenta - half_step * grad_zero
        moved = coords + step_size * half
        grad_one, curve_one = self.forces(moved, bias, amplitude)
        landed = half - half_step * grad_one
        self.first = join(moved, landed)[steps : steps + 1]
        coords, momenta = coords[:steps], momenta[:steps]
        self.curve_zero, self.curve_one = curve_zero[:steps], curve_one[:steps]
        self.moved, self.landed = moved[:steps], landed[:steps]
        self.start_q, self.start_p = coords[:1], momenta[:1]
        inside = iota((steps, 1), 0) < steps - 1

        def later(value):
            return jnp.where(inside, pltpu.roll(value, steps - 1, 0), 0.0)

        self.curve_next = later(self.curve_zero)
        self.off_q = self.moved - later(coords)
        off_p = self.landed - later(momenta)
        pulled = jnp.where(inside, self.off_q, 0.0)
        kicked = self.apart(self.along(pulled) * self.curve_next) + curvature * pulled
        self.off_p = off_p - half_step * kicked

    def along(self, value):
        left = mixed(value)
        return dot(jnp.concatenate([left, left], axis=1), self.onto)

    def apart(self, value):
        state = self.state
        high, low = split(value)
        out = dot(high, self.back) + dot(low, self.back)
        return out[:, :state] + out[:, state:]

    def forces(self, coords, bias, amplitude):
        gate = 1.0 / (1.0 + jnp.exp(-(self.along(coords) + bias)))
        pull = amplitude * gate
        return self.apart(pull) + curvature * coords, pull * (1.0 - gate)

    def hessians(self, curves, diagonal):
        count = curves.shape[0]
        width, state = self.width, self.state
        across = self.across[:width]
        scaled = [across * curves[k : k + 1] for k in range(count)]
        parts = [split(value) for value in scaled]
        stacked = jnp.concatenate([p[0] for p in parts] + [p[1] for p in parts], axis=0)
        out = dot(stacked, self.back)
        out = out[:, :state] + out[:, state:]
        out = out[: count * width] + out[count * width :]
        unit = jnp.where(iota((width, state), 0) == iota((width, state), 1) % width, 1.0, 0.0)
        found = []
        for k in range(count):
            high, low = split(out[k * width : (k + 1) * width] + diagonal[k] * unit)
            found.append(jnp.concatenate([high, high, low, low], axis=0))
        return found


def kick(coords, kicks):
    left = mixed(coords)
    return half_step * dot(jnp.concatenate([left, left], axis=1), kicks)


def window_map(local, kicks, opening):
    steps, state = local.steps, local.state
    runs = 4
    length = steps // runs
    ident = identity(state)
    maps = []
    states = []
    for c in range(runs):
        coords, momenta = twice(ident)
        if c == 0:
            coords, momenta = with_tail(coords, -local.start_q), with_tail(momenta, -local.start_p)
            momenta = momenta - kick(coords, opening)
        states.append((coords, momenta))
    for j in range(length):
        for c in range(runs):
            t = c * length + j
            coords, momenta = states[c]
            coords = coords + step_size * momenta
            momenta = momenta - kick(coords, kicks[t])
            states[c] = (
                with_tail(coords, local.off_q[t : t + 1]),
                with_tail(momenta, local.off_p[t : t + 1]),
            )
    return chain([join(*s) for s in states])


def kernel(
    sizes, guess_ref, start_ref, weight_ref, bias_ref, amplitude_ref, out_ref,
    kicks_ref, open_ref, offs_ref, rows_ref, core_ref, subs_ref, majors_ref, groups_ref,
    pre_ref, run_ref, vector_ref, spread_ref,
    core_sems, subs_send, subs_recv, majors_send, majors_recv, groups_send, groups_recv,
    pre_sems, spread_send, vector_recv, tokens,
):
    n_tm, n_sub, n_inner = sizes
    n_groups = n_tm // planes
    part, tm = lax.axis_index("parts"), lax.axis_index("tm")
    sub, inner = lax.axis_index("sub"), lax.axis_index("inner")
    group, plane = lax.div(tm, planes), lax.rem(tm, planes)
    middle = planes // 2
    state = guess_ref.shape[1]
    steps = guess_ref.shape[0]
    last = n_inner - 1
    lead = inner == last
    head = jnp.logical_and(lead, plane == middle)
    serves = jnp.logical_and(head, lax.rem(group, n_sub) == sub)
    serving_sub = lax.rem(group, n_sub)

    def place(tm_at=None, sub_at=None, inner_at=None):
        return (
            part,
            tm if tm_at is None else tm_at,
            sub if sub_at is None else sub_at,
            inner if inner_at is None else inner_at,
        )

    barrier = pltpu.get_barrier_semaphore()

    def greet(where):
        pl.semaphore_signal(barrier, inc=1, device_id=where, device_id_type=MESH)

    group_up = lax.rem(group + 1, n_groups) * planes + middle
    group_down = lax.rem(group + n_groups - 1, n_groups) * planes + middle

    greet(place(inner_at=n_inner - 1 - inner))

    @pl.when(jnp.logical_not(serves))
    def _():
        greet(place(group * planes + middle, serving_sub, last))

    @pl.when(lead)
    def _():
        for k in range(1, n_sub):
            greet(place(sub_at=lax.rem(sub + k, n_sub)))

    @pl.when(head)
    def _():
        for k in range(1, planes):
            greet(place(group * planes + lax.rem(middle + k, planes)))
        greet(place(group_up))
        greet(place(group_down))

    local = Local(
        guess_ref[...], start_ref[...], weight_ref[...], bias_ref[...], amplitude_ref[...]
    )
    diagonal = [2.0 * curvature] * (steps - 1) + [curvature, curvature]
    curves = jnp.concatenate(
        [local.curve_one + local.curve_next, jnp.broadcast_to(local.curve_zero[:1], (tail, local.curve_zero.shape[1]))],
        axis=0,
    )[: steps + 1]
    found = local.hessians(curves, diagonal)
    window = window_map(local, found[:steps], found[steps])
    own_ref = run_ref
    own_ref[...] = window

    for t in range(steps):
        kicks_ref[t, :, :state] = found[t]
    open_ref[...] = found[steps]
    offs_ref[0] = local.off_q
    offs_ref[1] = local.off_p
    rows_ref[0] = local.moved
    rows_ref[1] = local.landed
    first = local.first
    start_q, start_p = local.start_q, local.start_p

    count = jnp.where(lead, n_sub, 1) + jnp.where(lead, jnp.where(head, 2, 1), 0)
    count = count + jnp.where(serves, planes * n_sub * n_inner - 1, 0)
    pl.semaphore_wait(barrier, count)

    rounds = list(range(2, n_groups // 2 + 1))

    def tell(r):
        for where in (place(group_up), place(group_down)):
            pl.semaphore_signal(tokens.at[r - 2], inc=1, device_id=where, device_id_type=MESH)

    def hear(position):
        if position < len(rounds):
            pl.semaphore_wait(tokens.at[rounds[position] - 2], 2)
            if position + 1 < len(rounds):
                tell(rounds[position + 1])

    def copy(source, target, send, recv, where):
        return pltpu.make_async_remote_copy(
            src_ref=source, dst_ref=target, send_sem=send, recv_sem=recv,
            device_id=where, device_id_type=MESH,
        )

    if rounds:
        @pl.when(head)
        def _():
            tell(rounds[0])

    to_lead = copy(own_ref, core_ref, core_sems.at[0], core_sems.at[1], place(inner_at=last))

    @pl.when(jnp.logical_not(lead))
    def _():
        to_lead.start()

    @pl.when(lead)
    def _():
        to_lead.wait_recv()
        subs_ref[sub] = compose(core_ref[...], own_ref[...])
        for k in range(1, n_sub):
            copy(
                subs_ref.at[sub], subs_ref.at[sub], subs_send.at[k - 1], subs_recv.at[sub],
                place(sub_at=lax.rem(sub + k, n_sub)),
            ).start()

        @pl.when(head)
        def _():
            hear(0)

        for k in range(1, n_sub):
            other = lax.rem(sub + k, n_sub)
            copy(
                subs_ref.at[other], subs_ref.at[other], subs_send.at[k - 1], subs_recv.at[other],
                place(sub_at=other),
            ).wait_recv()
        majors_ref[plane] = chain([subs_ref[k] for k in range(n_sub)])

        @pl.when(jnp.logical_not(head))
        def _():
            copy(
                majors_ref.at[plane], majors_ref.at[plane], majors_send, majors_recv.at[plane],
                place(group * planes + middle),
            ).start()

        @pl.when(head)
        def _():
            hear(1)
            for k in range(planes):
                if k != middle:
                    copy(
                        majors_ref.at[k], majors_ref.at[k], majors_send, majors_recv.at[k],
                        place(group * planes + k),
                    ).wait_recv()
            groups_ref[group] = chain([majors_ref[k] for k in range(planes)])
            for position in range(2, max(3, len(rounds))):
                hear(position)
            for m in range(-(-n_groups // n_sub)):
                to = m * n_sub + sub

                @pl.when(jnp.logical_and(to > group, to < n_groups))
                def _():
                    copy(
                        groups_ref.at[group], groups_ref.at[group], groups_send.at[m],
                        groups_recv.at[group], place(to * planes + middle),
                    ).start()

        pre_ref[...] = identity(state)
        for k in range(n_sub - 1):
            @pl.when(k < sub)
            def _():
                pre_ref[...] = compose(pre_ref[...], subs_ref[k])

    to_other = copy(pre_ref, pre_ref, pre_sems.at[0], pre_sems.at[1], place(inner_at=0))

    @pl.when(lead)
    def _():
        to_other.start()

    @pl.when(jnp.logical_not(lead))
    def _():
        to_lead.wait_send()
        to_other.wait_recv()
        own_ref[...] = pre_ref[...]

    @pl.when(lead)
    def _():
        own_ref[...] = compose(pre_ref[...], core_ref[...])

    plain = local.hessians(local.curve_one, [curvature] * steps)
    for t in range(steps):
        kicks_ref[t, :, state:] = plain[t]

    coords, momenta = twice(own_ref[...])
    coords, momenta = with_tail(coords, -start_q), with_tail(momenta, -start_p)
    momenta = momenta - kick(coords, open_ref[...])
    maps_ref = spread_ref

    def advance(t, carry):
        coords, momenta = carry
        coords = coords + step_size * momenta
        both = kick(coords, kicks_ref[t])
        row = pl.ds(t, 1)
        maps_ref[t] = join(
            with_tail(coords, rows_ref[0, row, :]),
            with_tail(momenta - both[:, state:], rows_ref[1, row, :]),
        )
        return (
            with_tail(coords, offs_ref[0, row, :]),
            with_tail(momenta - both[:, :state], offs_ref[1, row, :]),
        )

    lax.fori_loop(0, steps - 1, advance, (coords, momenta))

    @pl.when(serves)
    def _():
        vector_ref[0] = jnp.broadcast_to(first, (tail, state))
        for k in range(n_groups - 1):
            @pl.when(k < group)
            def _():
                copy(
                    groups_ref.at[k], groups_ref.at[k], groups_send.at[0], groups_recv.at[k],
                    place(k * planes + middle),
                ).wait_recv()
                vector_ref[0] = jnp.broadcast_to(
                    applied(vector_ref[0, :1, :], groups_ref[k]), (tail, state)
                )
        entering = [vector_ref[0, :1, :]]
        for k in range(planes - 1):
            entering.append(applied(entering[-1], majors_ref[k]))
        for k in range(planes):
            vector_ref[1 + k] = jnp.broadcast_to(entering[k], (tail, state))

    def to_each(act):
        for k in range(planes):
            for s in range(n_sub):
                for c in range(n_inner):
                    at = (k * n_sub + s) * n_inner + c

                    def go(k=k, s=s, c=c, at=at):
                        act(copy(
                            vector_ref.at[1 + k], vector_ref.at[1 + planes],
                            spread_send_sems.at[at], vector_recv,
                            place(group * planes + k, s, c),
                        ))

                    if k == middle and c == last:
                        pl.when(s != sub)(go)
                    else:
                        go()

    spread_send_sems = spread_send

    @pl.when(serves)
    def _():
        to_each(lambda c: c.start())
        vector_ref[1 + planes] = vector_ref[1 + middle]

    @pl.when(jnp.logical_not(serves))
    def _():
        copy(
            vector_ref.at[1], vector_ref.at[1 + planes], spread_send.at[0], vector_recv,
            place(group * planes + middle, serving_sub, last),
        ).wait_recv()

    vector = vector_ref[1 + planes, :1, :]
    eye = iota((state, state), 0) == iota((state, state), 1)
    column = jnp.sum(jnp.where(eye, vector, 0.0), axis=1, keepdims=True)
    for t in range(steps):
        ref = own_ref if t == 0 else maps_ref.at[t - 1]
        out_ref[t : t + 1, :] = (
            jnp.sum(column * ref[:state, :], axis=0, keepdims=True) + ref[state : state + 1, :]
        )

    @pl.when(lead)
    def _():
        for k in range(1, n_sub):
            copy(
                subs_ref.at[sub], subs_ref.at[sub], subs_send.at[k - 1], subs_recv.at[sub],
                place(sub_at=lax.rem(sub + k, n_sub)),
            ).wait_send()
        to_other.wait_send()

        @pl.when(jnp.logical_not(head))
        def _():
            copy(
                majors_ref.at[plane], majors_ref.at[plane], majors_send, majors_recv.at[plane],
                place(group * planes + middle),
            ).wait_send()

        @pl.when(head)
        def _():
            for m in range(-(-n_groups // n_sub)):
                to = m * n_sub + sub

                @pl.when(jnp.logical_and(to > group, to < n_groups))
                def _():
                    copy(
                        groups_ref.at[group], groups_ref.at[group], groups_send.at[m],
                        groups_recv.at[group], place(to * planes + middle),
                    ).wait_send()

    @pl.when(serves)
    def _():
        to_each(lambda c: c.wait_send())


def shards(sizes, guess, start, layer_weight, layer_bias, amplitude):
    n_tm, n_sub, n_inner = sizes
    steps, state = guess.shape
    rows = state + tail
    n_groups = n_tm // planes
    vmem = pl.BlockSpec(memory_space=pltpu.VMEM)
    dma, regular = pltpu.SemaphoreType.DMA, pltpu.SemaphoreType.REGULAR
    return pl.pallas_call(
        functools.partial(kernel, sizes),
        out_shape=jax.ShapeDtypeStruct((steps, state), f32),
        in_specs=[vmem] * 5,
        out_specs=vmem,
        scratch_shapes=[
            pltpu.VMEM((steps, 2 * state, 2 * state), bf16),
            pltpu.VMEM((2 * state, state), bf16),
            pltpu.VMEM((2, steps, state), f32),
            pltpu.VMEM((2, steps, state), f32),
            pltpu.VMEM((rows, state), f32),
            pltpu.VMEM((n_sub, rows, state), f32),
            pltpu.VMEM((planes, rows, state), f32),
            pltpu.VMEM((n_groups, rows, state), f32),
            pltpu.VMEM((rows, state), f32),
            pltpu.VMEM((rows, state), f32),
            pltpu.VMEM((2 + planes, tail, state), f32),
            pltpu.VMEM((steps, rows, state), f32),
            dma((2,)),
            dma((n_sub,)),
            dma((n_sub,)),
            dma,
            dma((planes,)),
            dma((-(-n_groups // n_sub),)),
            dma((n_groups,)),
            dma((2,)),
            dma((planes * n_sub * n_inner,)),
            dma,
            regular((max(1, n_groups // 2),)),
        ],
        compiler_params=pltpu.CompilerParams(collective_id=0, has_side_effects=True),
    )(guess, start.reshape(1, -1), layer_weight, layer_bias.reshape(1, -1), amplitude.reshape(1, -1))


def solution(mesh):
    sizes = tuple(mesh.shape[name] for name in ("tm", "sub", "inner"))
    placed = (P(("parts", "tm", "sub", "inner"), None), P("parts"), P(), P(), P())
    return jax.shard_map(
        functools.partial(shards, sizes),
        mesh=mesh,
        in_specs=placed,
        out_specs=P(("parts", "tm", "sub", "inner"), None),
        check_vma=False,
    )
```

time: 319 us -> 66.8 us (0.21)
  the two profiles are of different devices: /device:TPU:34 before, /device:TPU:33 now
where the time goes in v1:
time: 66.8 us; the launch traced here: 66.6 us
  Pallas kernels  63.7 us (95%)
  local copies, waits for them, and re-layouts  2.87 us (4%)
    pallas_call x1, Pallas kernels, shards(): pl.pallas_call(functools.partial(kernel, sizes), out_shape=jax.ShapeDtype...  63.7 us
    unnamed x2, local copies, waits for them, and re-layouts  2.87 us

profile of v1, /device:TPU:33, one launch (start us, length us, event | category | flops | bytes accessed | tf_op | source)
XLA Modules:
  0.0 66.6 jit_solution(7318701901692068672)
XLA Ops:
  0.0 1.6 %copy.6.weight_ref = f32[256,64]{1,0:T(8,128)} copy(f32[256,64]{0,1:T(8,128)} %param.7) | data formatting | bytes 131072 | tf_op args[2]
  1.6 63.7 %shard_map.55 = f32[16,128]{1,0:T(8,128)} custom-call(f32[16,128]{1,0:T(8,128)} %guess_ref.1, f32[1,128]{1,0:T(1,128)} %bitcast.5, f32[256,64]{1,0:T(8,128)} %copy.6.weight_ref, f32[1,256]{1,0:T(1,128)} %bitcast.3, f32[1,256]{1,0:T(1,128)} %bitcast.4), custom_call_target="tpu_custom_call" | custom-call | tf_op jit(solution)/shard_map/pallas_call | solution.py:496
  65.3 1.3 %copy.8 = f32[16,128]{1,0:T(8,128)} copy(f32[16,128]{1,0:T(8,128)} %shard_map.55) | data formatting | bytes 16384

commit v2 on v1

v2 whole, which is shorter than its diff:
```python
import functools

import jax
import jax.numpy as jnp
from jax import lax
from jax.experimental import pallas as pl
from jax.experimental.pallas import tpu as pltpu
from jax.sharding import PartitionSpec as P

step_size = 0.04
curvature = 0.5
half_step = 0.5 * step_size
f32, bf16 = jnp.float32, jnp.bfloat16
MESH = pl.DeviceIdType.MESH
planes = 4
tail = 8


def iota(shape, axis):
    return lax.broadcasted_iota(jnp.int32, shape, axis)


def split(value):
    high = value.astype(bf16)
    return high, (value - high.astype(f32)).astype(bf16)


def low_lanes(value):
    width = value.shape[-1]
    return iota(value.shape, 1) < width // 2


def mixed(value):
    high = value.astype(bf16).astype(f32)
    return jnp.where(low_lanes(value), high, value - high).astype(bf16)


def twice(value):
    swapped = pltpu.roll(value, value.shape[-1] // 2, 1)
    low = low_lanes(value)
    return jnp.where(low, value, swapped), jnp.where(low, swapped, value)


def join(coords, momenta):
    return jnp.where(low_lanes(coords), coords, momenta)


def dot(left, right):
    return jnp.dot(left, right, preferred_element_type=f32)


def with_tail(value, extra):
    rows = value.shape[0] - tail
    return jnp.concatenate([value[:rows], value[rows:] + extra], axis=0)


def compose(first, second):
    state = first.shape[1]
    eye = (iota((state, state), 0) == iota((state, state), 1)).astype(f32)
    high, low = split(second[:state] - eye)
    both = jnp.concatenate([high, low], axis=1)
    left = jnp.concatenate(split(first), axis=1)
    out = dot(left, jnp.concatenate([both, both], axis=0))
    return with_tail(first + (out[:, :state] + out[:, state:]), second[state:])


def chain(maps):
    while len(maps) > 1:
        maps = [
            compose(maps[k], maps[k + 1]) if k + 1 < len(maps) else maps[k]
            for k in range(0, len(maps), 2)
        ]
    return maps[0]


def identity(state):
    rows = state + tail
    return (iota((rows, state), 0) == iota((rows, state), 1)).astype(f32)


def applied(vector, full):
    state = vector.shape[1]
    eye = iota((state, state), 0) == iota((state, state), 1)
    column = jnp.sum(jnp.where(eye, vector, 0.0), axis=1, keepdims=True)
    return jnp.sum(column * full[:state], axis=0, keepdims=True) + full[state : state + 1]


class Local:
    def __init__(self, guess, start, weight, bias, amplitude):
        self.steps, self.state = guess.shape
        steps = self.steps
        self.across = jnp.concatenate([weight, weight], axis=0)
        doubled = self.across.T
        high, low = split(self.across)
        self.onto = jnp.concatenate([high, low], axis=0)
        high, low = split(doubled)
        self.back = jnp.concatenate([high, low], axis=1)
        self.width = self.state // 2
        rows = jnp.concatenate([guess, jnp.broadcast_to(start, (tail, self.state))], axis=0)
        coords, momenta = twice(rows)
        grad_zero, curve_zero = self.forces(coords, bias, amplitude)
        half = momenta - half_step * grad_zero
        moved = coords + step_size * half
        grad_one, curve_one = self.forces(moved, bias, amplitude)
        landed = half - half_step * grad_one
        self.first = join(moved, landed)[steps : steps + 1]
        coords, momenta = coords[:steps], momenta[:steps]
        self.curve_zero, self.curve_one = curve_zero[:steps], curve_one[:steps]
        self.moved, self.landed = moved[:steps], landed[:steps]
        self.start_q, self.start_p = coords[:1], momenta[:1]
        inside = iota((steps, 1), 0) < steps - 1

        def later(value):
            return jnp.where(inside, pltpu.roll(value, steps - 1, 0), 0.0)

        self.curve_next = later(self.curve_zero)
        self.off_q = self.moved - later(coords)
        off_p = self.landed - later(momenta)
        pulled = jnp.where(inside, self.off_q, 0.0)
        kicked = self.apart(self.along(pulled) * self.curve_next) + curvature * pulled
        self.off_p = off_p - half_step * kicked

    def along(self, value):
        left = mixed(value)
        return dot(jnp.concatenate([left, left], axis=1), self.onto)

    def apart(self, value):
        state = self.state
        high, low = split(value)
        out = dot(high, self.back) + dot(low, self.back)
        return out[:, :state] + out[:, state:]

    def forces(self, coords, bias, amplitude):
        gate = 1.0 / (1.0 + jnp.exp(-(self.along(coords) + bias)))
        pull = amplitude * gate
        return self.apart(pull) + curvature * coords, pull * (1.0 - gate)

    def hessians(self, curves, diagonal):
        count = curves.shape[0]
        width, state = self.width, self.state
        across = self.across[:width]
        scaled = [across * curves[k : k + 1] for k in range(count)]
        parts = [split(value) for value in scaled]
        stacked = jnp.concatenate([p[0] for p in parts] + [p[1] for p in parts], axis=0)
        out = dot(stacked, self.back)
        out = out[:, :state] + out[:, state:]
        out = out[: count * width] + out[count * width :]
        unit = jnp.where(iota((width, state), 0) == iota((width, state), 1) % width, 1.0, 0.0)
        found = []
        for k in range(count):
            high, low = split(out[k * width : (k + 1) * width] + diagonal[k] * unit)
            found.append(jnp.concatenate([high, high, low, low], axis=0))
        return found


def kick(coords, kicks):
    left = mixed(coords)
    return half_step * dot(jnp.concatenate([left, left], axis=1), kicks)


def window_map(local, kicks, opening):
    steps, state = local.steps, local.state
    runs = 4
    length = steps // runs
    ident = identity(state)
    maps = []
    states = []
    for c in range(runs):
        coords, momenta = twice(ident)
        if c == 0:
            coords, momenta = with_tail(coords, -local.start_q), with_tail(momenta, -local.start_p)
            momenta = momenta - kick(coords, opening)
        states.append((coords, momenta))
    for j in range(length):
        for c in range(runs):
            t = c * length + j
            coords, momenta = states[c]
            coords = coords + step_size * momenta
            momenta = momenta - kick(coords, kicks[t])
            states[c] = (
                with_tail(coords, local.off_q[t : t + 1]),
                with_tail(momenta, local.off_p[t : t + 1]),
            )
    return chain([join(*s) for s in states])


def kernel(
    sizes, guess_ref, start_ref, weight_ref, bias_ref, amplitude_ref, out_ref,
    kicks_ref, open_ref, offs_ref, rows_ref, core_ref, subs_ref, majors_ref, ahead_ref,
    pre_ref, run_ref, vector_ref, maps_ref,
    core_sems, subs_send, subs_recv, majors_send, majors_recv, pre_sems,
    spread_send, vector_recv, entry_send, entry_recv,
):
    n_tm, n_sub, n_inner = sizes
    n_groups = n_tm // planes
    part, tm = lax.axis_index("parts"), lax.axis_index("tm")
    sub, inner = lax.axis_index("sub"), lax.axis_index("inner")
    group, plane = lax.div(tm, planes), lax.rem(tm, planes)
    steps, state = guess_ref.shape
    last = n_inner - 1
    lead = inner == last
    other = jnp.logical_not(lead)
    column = jnp.logical_and(lead, sub == 0)
    head = jnp.logical_and(column, plane == 0)
    opening_chip = jnp.logical_and(tm == 0, sub == 0)
    origin = jnp.logical_and(opening_chip, inner == 0)

    def place(tm_at=None, sub_at=None, inner_at=None):
        return (
            part,
            tm if tm_at is None else tm_at,
            sub if sub_at is None else sub_at,
            inner if inner_at is None else inner_at,
        )

    def copy(source, target, send, recv, where):
        return pltpu.make_async_remote_copy(
            src_ref=source, dst_ref=target, send_sem=send, recv_sem=recv,
            device_id=where, device_id_type=MESH,
        )

    def both(*conditions):
        return functools.reduce(jnp.logical_and, conditions)

    barrier = pltpu.get_barrier_semaphore()

    def greet(where):
        pl.semaphore_signal(barrier, inc=1, device_id=where, device_id_type=MESH)

    @pl.when(jnp.logical_not(origin))
    def _():
        @pl.when(jnp.logical_not(both(opening_chip, lead)))
        def _():
            greet(place(inner_at=n_inner - 1 - inner))

        @pl.when(tm == 0)
        def _():
            greet(place(0, 0, 0))

        @pl.when(both(tm > 0, jnp.logical_not(head)))
        def _():
            greet(place(group * planes, 0, last))

    def takes_from(s):
        return both(lead, sub != s, jnp.logical_or(sub > s, sub == 0))

    def gives_to(t):
        return both(lead, sub != t, jnp.logical_or(sub < t, t == 0))

    for s in range(n_sub):
        @pl.when(takes_from(s))
        def _():
            greet(place(sub_at=s))

    @pl.when(head)
    def _():
        for k in range(1, planes):
            greet(place(group * planes + k))

        @pl.when(group > 0)
        def _():
            greet(place((group - 1) * planes))

    local = Local(
        guess_ref[...], start_ref[...], weight_ref[...], bias_ref[...], amplitude_ref[...]
    )
    diagonal = [2.0 * curvature] * (steps - 1) + [curvature, curvature]
    curves = jnp.concatenate(
        [
            local.curve_one + local.curve_next,
            jnp.broadcast_to(local.curve_zero[:1], (tail, local.curve_zero.shape[1])),
        ],
        axis=0,
    )[: steps + 1]
    found = local.hessians(curves, diagonal)
    run_ref[...] = window_map(local, found[:steps], found[steps])
    first = local.first
    start_q, start_p = local.start_q, local.start_p

    count = jnp.where(jnp.logical_and(lead, jnp.logical_not(opening_chip)), 1, 0)
    count = count + jnp.where(other, 1, 0)
    count = count + jnp.where(lead, jnp.where(sub == 0, n_sub - 1, n_sub - sub), 0)
    count = count + jnp.where(jnp.logical_and(column, plane > 0), 1, 0)
    around = n_sub * n_inner
    count = count + jnp.where(head, (planes - 1) * around, 0)
    count = count + jnp.where(jnp.logical_and(head, group > 0), around - 1, 0)
    count = count + jnp.where(jnp.logical_and(head, group < n_groups - 1), 1, 0)
    count = jnp.where(origin, around - 1, count)
    pl.semaphore_wait(barrier, count)

    entry, arrived, onward = 0, planes + 1, planes + 2
    entering = vector_ref.at[entry]

    def from_origin(act):
        for s in range(n_sub):
            for c in range(n_inner):
                if (s, c) == (0, 0):
                    continue
                ahead = (s, c) == (0, last)
                act(copy(
                    vector_ref.at[onward],
                    entering if ahead else vector_ref.at[arrived],
                    spread_send.at[s * n_inner + c],
                    entry_recv if ahead else vector_recv,
                    place(0, s, c),
                ))

    @pl.when(origin)
    def _():
        vector_ref[onward] = jnp.broadcast_to(applied(first, run_ref), (tail, state))
        from_origin(lambda c: c.start())
        vector_ref[arrived] = jnp.broadcast_to(first, (tail, state))

    for t in range(steps):
        kicks_ref[t, :, :state] = found[t]
    open_ref[...] = found[steps]
    offs_ref[0] = local.off_q
    offs_ref[1] = local.off_p
    rows_ref[0] = local.moved
    rows_ref[1] = local.landed
    plain = local.hessians(local.curve_one, [curvature] * steps)
    for t in range(steps):
        kicks_ref[t, :, state:] = plain[t]

    to_lead = copy(run_ref, core_ref, core_sems.at[0], core_sems.at[1], place(inner_at=last))
    to_other = copy(pre_ref, pre_ref, pre_sems.at[0], pre_sems.at[1], place(inner_at=0))
    to_head = copy(
        majors_ref.at[plane], majors_ref.at[plane], majors_send, majors_recv.at[plane],
        place(group * planes),
    )

    def to_sub(t):
        return copy(
            subs_ref.at[sub], subs_ref.at[sub], subs_send.at[t], subs_recv.at[sub],
            place(sub_at=t),
        )

    @pl.when(jnp.logical_and(other, jnp.logical_not(origin)))
    def _():
        to_lead.start()

    @pl.when(lead)
    def _():
        @pl.when(opening_chip)
        def _():
            subs_ref[sub] = run_ref[...]

        @pl.when(jnp.logical_not(opening_chip))
        def _():
            to_lead.wait_recv()
            subs_ref[sub] = compose(core_ref[...], run_ref[...])

        for t in range(n_sub):
            @pl.when(gives_to(t))
            def _():
                to_sub(t).start()

        for s in range(n_sub):
            @pl.when(takes_from(s))
            def _():
                copy(
                    subs_ref.at[s], subs_ref.at[s], subs_send.at[s], subs_recv.at[s],
                    place(sub_at=s),
                ).wait_recv()

        pre_ref[...] = identity(state)
        for k in range(n_sub - 1):
            @pl.when(k < sub)
            def _():
                pre_ref[...] = compose(pre_ref[...], subs_ref[k])

        @pl.when(jnp.logical_not(opening_chip))
        def _():
            to_other.start()
            run_ref[...] = compose(pre_ref[...], core_ref[...])

        @pl.when(opening_chip)
        def _():
            run_ref[...] = identity(state)

        @pl.when(sub == 0)
        def _():
            majors_ref[plane] = chain([subs_ref[k] for k in range(n_sub)])

            @pl.when(plane > 0)
            def _():
                to_head.start()

            @pl.when(plane == 0)
            def _():
                ahead_ref[0] = majors_ref[0]
                for k in range(1, planes):
                    copy(
                        majors_ref.at[k], majors_ref.at[k], majors_send, majors_recv.at[k],
                        place(group * planes + k),
                    ).wait_recv()
                    ahead_ref[k] = compose(ahead_ref[k - 1], majors_ref[k])

    @pl.when(other)
    def _():
        @pl.when(origin)
        def _():
            run_ref[...] = identity(state)

        @pl.when(jnp.logical_not(origin))
        def _():
            to_lead.wait_send()
            to_other.wait_recv()
            run_ref[...] = pre_ref[...]

    coords, momenta = twice(run_ref[...])
    coords, momenta = with_tail(coords, -start_q), with_tail(momenta, -start_p)
    momenta = momenta - kick(coords, open_ref[...])

    def advance(t, carry):
        coords, momenta = carry
        coords = coords + step_size * momenta
        pair = kick(coords, kicks_ref[t])
        row = pl.ds(t, 1)
        maps_ref[t] = join(
            with_tail(coords, rows_ref[0, row, :]),
            with_tail(momenta - pair[:, state:], rows_ref[1, row, :]),
        )
        return (
            with_tail(coords, offs_ref[0, row, :]),
            with_tail(momenta - pair[:, :state], offs_ref[1, row, :]),
        )

    lax.fori_loop(0, steps - 1, advance, (coords, momenta))

    def to_next(source):
        return copy(source, entering, entry_send, entry_recv, place((group + 1) * planes))

    def to_each(act):
        def send(k, s, c):
            act(copy(
                entering if k == 0 else vector_ref.at[k],
                vector_ref.at[arrived],
                spread_send.at[(k * n_sub + s) * n_inner + c],
                vector_recv,
                place(group * planes + k, s, c),
            ))

        for k in range(1, planes):
            for s in range(n_sub):
                for c in range(n_inner):
                    send(k, s, c)

        @pl.when(group > 0)
        def _():
            for s in range(n_sub):
                for c in range(n_inner):
                    if (s, c) != (0, last):
                        send(0, s, c)

    @pl.when(head)
    def _():
        to_next(vector_ref.at[onward]).wait_recv()
        here = vector_ref[entry, :1, :]
        for k in range(planes):
            slot = k + 1 if k + 1 < planes else onward
            vector_ref[slot] = jnp.broadcast_to(applied(here, ahead_ref[k]), (tail, state))
        to_each(lambda c: c.start())

        @pl.when(group < n_groups - 1)
        def _():
            to_next(vector_ref.at[onward]).start()

        vector_ref[arrived] = vector_ref[entry]

    @pl.when(both(jnp.logical_not(head), jnp.logical_not(origin)))
    def _():
        copy(
            vector_ref.at[entry], vector_ref.at[arrived], spread_send.at[0], vector_recv,
            place(group * planes, 0, last),
        ).wait_recv()

    vector = vector_ref[arrived, :1, :]
    eye = iota((state, state), 0) == iota((state, state), 1)
    upright = jnp.sum(jnp.where(eye, vector, 0.0), axis=1, keepdims=True)
    for t in range(steps):
        ref = run_ref if t == 0 else maps_ref.at[t - 1]
        out_ref[t : t + 1, :] = (
            jnp.sum(upright * ref[:state, :], axis=0, keepdims=True) + ref[state : state + 1, :]
        )

    @pl.when(origin)
    def _():
        from_origin(lambda c: c.wait_send())

    @pl.when(lead)
    def _():
        for t in range(n_sub):
            @pl.when(gives_to(t))
            def _():
                to_sub(t).wait_send()

        @pl.when(jnp.logical_not(opening_chip))
        def _():
            to_other.wait_send()

        @pl.when(jnp.logical_and(column, plane > 0))
        def _():
            to_head.wait_send()

    @pl.when(head)
    def _():
        to_each(lambda c: c.wait_send())

        @pl.when(group < n_groups - 1)
        def _():
            to_next(vector_ref.at[onward]).wait_send()


def shards(sizes, guess, start, layer_weight, layer_bias, amplitude):
    n_tm, n_sub, n_inner = sizes
    steps, state = guess.shape
    rows = state + tail
    vmem = pl.BlockSpec(memory_space=pltpu.VMEM)
    dma, regular = pltpu.SemaphoreType.DMA, pltpu.SemaphoreType.REGULAR
    return pl.pallas_call(
        functools.partial(kernel, sizes),
        out_shape=jax.ShapeDtypeStruct((steps, state), f32),
        in_specs=[vmem] * 5,
        out_specs=vmem,
        scratch_shapes=[
            pltpu.VMEM((steps, 2 * state, 2 * state), bf16),
            pltpu.VMEM((2 * state, state), bf16),
            pltpu.VMEM((2, steps, state), f32),
            pltpu.VMEM((2, steps, state), f32),
            pltpu.VMEM((rows, state), f32),
            pltpu.VMEM((n_sub, rows, state), f32),
            pltpu.VMEM((planes, rows, state), f32),
            pltpu.VMEM((planes, rows, state), f32),
            pltpu.VMEM((rows, state), f32),
            pltpu.VMEM((rows, state), f32),
            pltpu.VMEM((3 + planes, tail, state), f32),
            pltpu.VMEM((steps, rows, state), f32),
            dma((2,)),
            dma((n_sub,)),
            dma((n_sub,)),
            dma,
            dma((planes,)),
            dma((2,)),
            dma((planes * n_sub * n_inner,)),
            dma,
            dma,
            dma,
        ],
        compiler_params=pltpu.CompilerParams(collective_id=0, has_side_effects=True),
    )(guess, start.reshape(1, -1), layer_weight.T, layer_bias.reshape(1, -1), amplitude.reshape(1, -1))


def solution(mesh):
    sizes = tuple(mesh.shape[name] for name in ("tm", "sub", "inner"))
    placed = (P(("parts", "tm", "sub", "inner"), None), P("parts"), P(), P(), P())
    return jax.shard_map(
        functools.partial(shards, sizes),
        mesh=mesh,
        in_specs=placed,
        out_specs=P(("parts", "tm", "sub", "inner"), None),
        check_vma=False,
    )
```

time: 66.8 us -> 50.6 us (0.76)
  Pallas kernels: 63.7 us -> 49.1 us
  local copies, waits for them, and re-layouts: 2.87 us -> 1.3 us
    pallas_call x1, Pallas kernels: 63.7 us -> 49.1 us  [shards(): pl.pallas_call(functools.partial(kernel, sizes), out_shape=jax.ShapeDtype...]
    unnamed x2 -> x1, local copies, waits for them, and re-layouts: 2.87 us -> 1.3 us
where the time goes in v2:
time: 50.6 us; the launch traced here: 50.4 us
  Pallas kernels  49.1 us (97%)
  local copies, waits for them, and re-layouts  1.3 us (3%)
    pallas_call x1, Pallas kernels, shards(): pl.pallas_call(functools.partial(kernel, sizes), out_shape=jax.ShapeDtype...  49.1 us
    unnamed x1, local copies, waits for them, and re-layouts  1.3 us

profile of v2, /device:TPU:33, one launch (start us, length us, event | category | flops | bytes accessed | tf_op | source)
XLA Modules:
  0.0 50.4 jit_solution(11085045657088586966)
XLA Ops:
  0.0 49.1 %shard_map.55 = f32[16,128]{1,0:T(8,128)} custom-call(f32[16,128]{1,0:T(8,128)} %guess_ref.1, f32[1,128]{1,0:T(1,128)} %bitcast.7, f32[64,256]{1,0:T(8,128)} %bitcast.4, f32[1,256]{1,0:T(1,128)} %bitcast.5, f32[1,256]{1,0:T(1,128)} %bitcast.6), custom_call_target="tpu_custom_call" | custom-call | tf_op jit(solution)/shard_map/pallas_call | solution.py:521
  49.1 1.3 %copy.7 = f32[16,128]{1,0:T(8,128)} copy(f32[16,128]{1,0:T(8,128)} %shard_map.55) | data formatting | bytes 16384

commit v3 on v2

--- a/solution.py
+++ b/solution.py
@@ -51,6 +51,8 @@
 
 def with_tail(value, extra):
     rows = value.shape[0] - tail
+    if rows == 0:
+        return value + extra
     return jnp.concatenate([value[:rows], value[rows:] + extra], axis=0)
 
 
@@ -85,25 +87,65 @@
     return jnp.sum(column * full[:state], axis=0, keepdims=True) + full[state : state + 1]
 
 
-class Local:
-    def __init__(self, guess, start, weight, bias, amplitude):
-        self.steps, self.state = guess.shape
-        steps = self.steps
-        self.across = jnp.concatenate([weight, weight], axis=0)
-        doubled = self.across.T
-        high, low = split(self.across)
-        self.onto = jnp.concatenate([high, low], axis=0)
-        high, low = split(doubled)
-        self.back = jnp.concatenate([high, low], axis=1)
-        self.width = self.state // 2
-        rows = jnp.concatenate([guess, jnp.broadcast_to(start, (tail, self.state))], axis=0)
-        coords, momenta = twice(rows)
-        grad_zero, curve_zero = self.forces(coords, bias, amplitude)
+class Weights:
+    def __init__(self, across_ref, onto_ref, back_ref, bias_ref, amplitude_ref):
+        self.across_ref, self.onto_ref, self.back_ref = across_ref, onto_ref, back_ref
+        self.bias_ref, self.amplitude_ref = bias_ref, amplitude_ref
+
+    def fill(self, weight):
+        across = jnp.concatenate([weight, weight], axis=0)
+        high, low = split(across)
+        self.onto_ref[...] = jnp.concatenate([high, low], axis=0)
+        high, low = split(across.T)
+        self.back_ref[...] = jnp.concatenate([high, low], axis=1)
+
+    def along(self, value):
+        left = mixed(value)
+        return dot(jnp.concatenate([left, left], axis=1), self.onto_ref[...])
+
+    def apart(self, value):
+        back = self.back_ref[...]
+        state = back.shape[1] // 2
+        high, low = split(value)
+        out = dot(high, back) + dot(low, back)
+        return out[:, :state] + out[:, state:]
+
+    def forces(self, coords):
+        gate = 1.0 / (1.0 + jnp.exp(-(self.along(coords) + self.bias_ref[...])))
+        pull = self.amplitude_ref[...] * gate
+        return self.apart(pull) + curvature * coords, pull * (1.0 - gate)
+
+    def hessians(self, curves, diagonal):
+        count = curves.shape[0]
+        across, back = self.across_ref[...], self.back_ref[...]
+        width, state = across.shape[0], back.shape[1] // 2
+        parts = [split(across * curves[k : k + 1]) for k in range(count)]
+        stacked = jnp.concatenate([p[0] for p in parts] + [p[1] for p in parts], axis=0)
+        out = dot(stacked, back)
+        out = out[:, :state] + out[:, state:]
+        out = out[: count * width] + out[count * width :]
+        unit = jnp.where(iota((width, state), 0) == iota((width, state), 1) % width, 1.0, 0.0)
+        return [out[k * width : (k + 1) * width] + diagonal[k] * unit for k in range(count)]
+
+
+def stationary(hessian):
+    high, low = split(hessian)
+    return jnp.concatenate([high, high, low, low], axis=0)
+
+
+class Window:
+    def __init__(self, weights, rows, start):
+        self.steps, self.state = steps, state = rows.shape
+        coords, momenta = twice(
+            jnp.concatenate([rows, jnp.broadcast_to(start, (tail, state))], axis=0)
+        )
+        grad_zero, curve_zero = weights.forces(coords)
         half = momenta - half_step * grad_zero
         moved = coords + step_size * half
-        grad_one, curve_one = self.forces(moved, bias, amplitude)
+        grad_one, curve_one = weights.forces(moved)
         landed = half - half_step * grad_one
-        self.first = join(moved, landed)[steps : steps + 1]
+        self.first_q, self.first_p = moved[steps:], landed[steps:]
+        self.first = join(self.first_q, self.first_p)[:1]
         coords, momenta = coords[:steps], momenta[:steps]
         self.curve_zero, self.curve_one = curve_zero[:steps], curve_one[:steps]
         self.moved, self.landed = moved[:steps], landed[:steps]
@@ -113,44 +155,18 @@
         def later(value):
             return jnp.where(inside, pltpu.roll(value, steps - 1, 0), 0.0)
 
-        self.curve_next = later(self.curve_zero)
+        curve_next = later(self.curve_zero)
+        opening = jnp.broadcast_to(self.curve_zero[:1], (tail, self.curve_zero.shape[1]))
+        self.curves = jnp.concatenate([self.curve_one + curve_next, opening], axis=0)[: steps + 1]
+        self.diagonal = [2.0 * curvature] * (steps - 1) + [curvature, curvature]
         self.off_q = self.moved - later(coords)
-        off_p = self.landed - later(momenta)
-        pulled = jnp.where(inside, self.off_q, 0.0)
-        kicked = self.apart(self.along(pulled) * self.curve_next) + curvature * pulled
-        self.off_p = off_p - half_step * kicked
-
-    def along(self, value):
-        left = mixed(value)
-        return dot(jnp.concatenate([left, left], axis=1), self.onto)
-
-    def apart(self, value):
-        state = self.state
-        high, low = split(value)
-        out = dot(high, self.back) + dot(low, self.back)
-        return out[:, :state] + out[:, state:]
-
-    def forces(self, coords, bias, amplitude):
-        gate = 1.0 / (1.0 + jnp.exp(-(self.along(coords) + bias)))
-        pull = amplitude * gate
-        return self.apart(pull) + curvature * coords, pull * (1.0 - gate)
-
-    def hessians(self, curves, diagonal):
-        count = curves.shape[0]
-        width, state = self.width, self.state
-        across = self.across[:width]
-        scaled = [across * curves[k : k + 1] for k in range(count)]
-        parts = [split(value) for value in scaled]
-        stacked = jnp.concatenate([p[0] for p in parts] + [p[1] for p in parts], axis=0)
-        out = dot(stacked, self.back)
-        out = out[:, :state] + out[:, state:]
-        out = out[: count * width] + out[count * width :]
-        unit = jnp.where(iota((width, state), 0) == iota((width, state), 1) % width, 1.0, 0.0)
-        found = []
-        for k in range(count):
-            high, low = split(out[k * width : (k + 1) * width] + diagonal[k] * unit)
-            found.append(jnp.concatenate([high, high, low, low], axis=0))
-        return found
+        begin_q = self.first_q - self.start_q
+        begin_p = self.first_p - self.start_p
+        pulled = jnp.concatenate([jnp.where(inside, self.off_q, 0.0), begin_q], axis=0)
+        curve = jnp.concatenate([curve_next, opening], axis=0)
+        kicked = half_step * (weights.apart(weights.along(pulled) * curve) + curvature * pulled)
+        self.off_p = self.landed - later(momenta) - kicked[:steps]
+        self.begin_q, self.begin_p = begin_q, begin_p - kicked[steps:]
 
 
 def kick(coords, kicks):
@@ -158,18 +174,18 @@
     return half_step * dot(jnp.concatenate([left, left], axis=1), kicks)
 
 
-def window_map(local, kicks, opening):
-    steps, state = local.steps, local.state
+def window_map(window, kicks):
+    steps, state = window.steps, window.state
     runs = 4
     length = steps // runs
     ident = identity(state)
-    maps = []
     states = []
     for c in range(runs):
         coords, momenta = twice(ident)
         if c == 0:
-            coords, momenta = with_tail(coords, -local.start_q), with_tail(momenta, -local.start_p)
-            momenta = momenta - kick(coords, opening)
+            coords = with_tail(coords, -window.start_q)
+            momenta = with_tail(momenta, -window.start_p)
+            momenta = momenta - kick(coords, kicks[steps])
         states.append((coords, momenta))
     for j in range(length):
         for c in range(runs):
@@ -178,18 +194,57 @@
             coords = coords + step_size * momenta
             momenta = momenta - kick(coords, kicks[t])
             states[c] = (
-                with_tail(coords, local.off_q[t : t + 1]),
-                with_tail(momenta, local.off_p[t : t + 1]),
+                with_tail(coords, window.off_q[t : t + 1]),
+                with_tail(momenta, window.off_p[t : t + 1]),
             )
     return chain([join(*s) for s in states])
 
 
+def left_state(weights, rows, start):
+    window = Window(weights, rows, start)
+    steps, state = window.steps, window.state
+    width = state // 2
+    runs = 4
+    length = steps // runs
+    hessians = weights.hessians(window.curves, window.diagonal)
+    repeated = jnp.where(iota((width, state), 0) == iota((width, state), 1) % width, 1.0, 0.0)
+    none = jnp.zeros((tail, state), f32)
+    moving = jnp.concatenate([repeated, step_size * repeated, none], axis=0)
+    states = [(window.begin_q, window.begin_p)]
+    for c in range(1, runs):
+        t = c * length
+        bend = half_step * hessians[t]
+        momenta = jnp.concatenate([-bend, repeated - step_size * bend, none], axis=0)
+        states.append((
+            with_tail(moving, window.off_q[t : t + 1]),
+            with_tail(momenta, window.off_p[t : t + 1]),
+        ))
+    for j in range(length):
+        for c in range(runs):
+            if j == length - 1 and c > 0:
+                continue
+            t = c * length + j + (1 if c else 0)
+            coords, momenta = states[c]
+            coords = coords + step_size * momenta
+            momenta = momenta - kick(coords, stationary(hessians[t]))
+            states[c] = (
+                with_tail(coords, window.off_q[t : t + 1]),
+                with_tail(momenta, window.off_p[t : t + 1]),
+            )
+    maps = [join(*s) for s in states]
+    vector = maps[0][:1]
+    for full in maps[1:]:
+        vector = applied(vector, full)
+    return vector
+
+
 def kernel(
-    sizes, guess_ref, start_ref, weight_ref, bias_ref, amplitude_ref, out_ref,
+    sizes, guess_hbm, start_hbm, weight_hbm, bias_hbm, amplitude_hbm, out_ref,
+    guess_ref, start_ref, weight_ref, bias_ref, amplitude_ref,
     kicks_ref, open_ref, offs_ref, rows_ref, core_ref, subs_ref, majors_ref, ahead_ref,
-    pre_ref, run_ref, vector_ref, maps_ref,
+    pre_ref, run_ref, vector_ref, maps_ref, onto_ref, back_ref, raw_ref,
     core_sems, subs_send, subs_recv, majors_send, majors_recv, pre_sems,
-    spread_send, vector_recv, entry_send, entry_recv,
+    spread_send, vector_recv, entry_send, entry_recv, raw_recv, load_sems,
 ):
     n_tm, n_sub, n_inner = sizes
     n_groups = n_tm // planes
@@ -223,6 +278,36 @@
         return functools.reduce(jnp.logical_and, conditions)
 
     barrier = pltpu.get_barrier_semaphore()
+    around = n_sub * n_inner
+    loads = [
+        pltpu.make_async_copy(source, target, load_sems.at[k])
+        for k, (source, target) in enumerate((
+            (guess_hbm, guess_ref), (weight_hbm, weight_ref), (start_hbm, start_ref),
+            (bias_hbm, bias_ref), (amplitude_hbm, amplitude_ref),
+        ))
+    ]
+    for load in loads:
+        load.start()
+
+    def from_origin(act):
+        def send(at, carry):
+            act(copy(
+                guess_ref, raw_ref, spread_send.at[at], raw_recv,
+                place(0, lax.div(at, n_inner), lax.rem(at, n_inner)),
+            ))
+            return carry
+
+        lax.fori_loop(1, around, send, 0)
+
+    @pl.when(origin)
+    def _():
+        pl.semaphore_wait(barrier, around - 1)
+        loads[0].wait()
+        from_origin(lambda c: c.start())
+
+    @pl.when(jnp.logical_not(origin))
+    def _():
+        loads[0].wait()
 
     def greet(where):
         pl.semaphore_signal(barrier, inc=1, device_id=where, device_id_type=MESH)
@@ -261,66 +346,45 @@
         def _():
             greet(place((group - 1) * planes))
 
-    local = Local(
-        guess_ref[...], start_ref[...], weight_ref[...], bias_ref[...], amplitude_ref[...]
-    )
-    diagonal = [2.0 * curvature] * (steps - 1) + [curvature, curvature]
-    curves = jnp.concatenate(
-        [
-            local.curve_one + local.curve_next,
-            jnp.broadcast_to(local.curve_zero[:1], (tail, local.curve_zero.shape[1])),
-        ],
-        axis=0,
-    )[: steps + 1]
-    found = local.hessians(curves, diagonal)
-    run_ref[...] = window_map(local, found[:steps], found[steps])
-    first = local.first
-    start_q, start_p = local.start_q, local.start_p
+    for load in loads[1:]:
+        load.wait()
+    weights = Weights(weight_ref, onto_ref, back_ref, bias_ref, amplitude_ref)
+    weights.fill(weight_ref[...])
+    start = start_ref[...]
+    window = Window(weights, guess_ref[...], start)
+    found = [stationary(k) for k in weights.hessians(window.curves, window.diagonal)]
+    run_ref[...] = window_map(window, found)
+    start_q, start_p = window.start_q, window.start_p
 
     count = jnp.where(jnp.logical_and(lead, jnp.logical_not(opening_chip)), 1, 0)
     count = count + jnp.where(other, 1, 0)
     count = count + jnp.where(lead, jnp.where(sub == 0, n_sub - 1, n_sub - sub), 0)
     count = count + jnp.where(jnp.logical_and(column, plane > 0), 1, 0)
-    around = n_sub * n_inner
     count = count + jnp.where(head, (planes - 1) * around, 0)
     count = count + jnp.where(jnp.logical_and(head, group > 0), around - 1, 0)
     count = count + jnp.where(jnp.logical_and(head, group < n_groups - 1), 1, 0)
-    count = jnp.where(origin, around - 1, count)
-    pl.semaphore_wait(barrier, count)
+
+    @pl.when(jnp.logical_not(origin))
+    def _():
+        pl.semaphore_wait(barrier, count)
 
     entry, arrived, onward = 0, planes + 1, planes + 2
     entering = vector_ref.at[entry]
 
-    def from_origin(act):
-        for s in range(n_sub):
-            for c in range(n_inner):
-                if (s, c) == (0, 0):
-                    continue
-                ahead = (s, c) == (0, last)
-                act(copy(
-                    vector_ref.at[onward],
-                    entering if ahead else vector_ref.at[arrived],
-                    spread_send.at[s * n_inner + c],
-                    entry_recv if ahead else vector_recv,
-                    place(0, s, c),
-                ))
-
     @pl.when(origin)
     def _():
-        vector_ref[onward] = jnp.broadcast_to(applied(first, run_ref), (tail, state))
-        from_origin(lambda c: c.start())
-        vector_ref[arrived] = jnp.broadcast_to(first, (tail, state))
+        vector_ref[arrived] = jnp.broadcast_to(window.first, (tail, state))
 
     for t in range(steps):
         kicks_ref[t, :, :state] = found[t]
     open_ref[...] = found[steps]
-    offs_ref[0] = local.off_q
-    offs_ref[1] = local.off_p
-    rows_ref[0] = local.moved
-    rows_ref[1] = local.landed
-    plain = local.hessians(local.curve_one, [curvature] * steps)
+    offs_ref[0] = window.off_q
+    offs_ref[1] = window.off_p
+    rows_ref[0] = window.moved
+    rows_ref[1] = window.landed
+    plain = weights.hessians(window.curve_one, [curvature] * steps)
     for t in range(steps):
-        kicks_ref[t, :, state:] = plain[t]
+        kicks_ref[t, :, state:] = stationary(plain[t])
 
     to_lead = copy(run_ref, core_ref, core_sems.at[0], core_sems.at[1], place(inner_at=last))
     to_other = copy(pre_ref, pre_ref, pre_sems.at[0], pre_sems.at[1], place(inner_at=0))
@@ -432,43 +496,51 @@
         return copy(source, entering, entry_send, entry_recv, place((group + 1) * planes))
 
     def to_each(act):
-        def send(k, s, c):
-            act(copy(
-                entering if k == 0 else vector_ref.at[k],
-                vector_ref.at[arrived],
-                spread_send.at[(k * n_sub + s) * n_inner + c],
-                vector_recv,
-                place(group * planes + k, s, c),
-            ))
-
-        for k in range(1, planes):
-            for s in range(n_sub):
-                for c in range(n_inner):
-                    send(k, s, c)
-
+        def send(at, carry):
+            @pl.when(at != last)
+            def _():
+                k = lax.div(at, around)
+                act(copy(
+                    vector_ref.at[k], vector_ref.at[arrived], spread_send.at[at], vector_recv,
+                    place(
+                        group * planes + k,
+                        lax.rem(lax.div(at, n_inner), n_sub),
+                        lax.rem(at, n_inner),
+                    ),
+                ))
+
+            return carry
+
+        lax.fori_loop(jnp.where(group > 0, 0, around), planes * around, send, 0)
+
+    late = jnp.logical_and(tm == 0, jnp.logical_not(origin))
+
+    @pl.when(late)
+    def _():
+        copy(guess_ref, raw_ref, spread_send.at[0], raw_recv, place(0, 0, 0)).wait_recv()
+        left = jnp.broadcast_to(left_state(weights, raw_ref[...], start_ref[...]), (tail, state))
+        vector_ref[entry] = left
+        vector_ref[arrived] = left
+
+    @pl.when(head)
+    def _():
         @pl.when(group > 0)
         def _():
-            for s in range(n_sub):
-                for c in range(n_inner):
-                    if (s, c) != (0, last):
-                        send(0, s, c)
-
-    @pl.when(head)
-    def _():
-        to_next(vector_ref.at[onward]).wait_recv()
+            to_next(vector_ref.at[onward]).wait_recv()
+
         here = vector_ref[entry, :1, :]
         for k in range(planes):
             slot = k + 1 if k + 1 < planes else onward
             vector_ref[slot] = jnp.broadcast_to(applied(here, ahead_ref[k]), (tail, state))
+
+        @pl.when(group < n_groups - 1)
+        def _():
+            to_next(vector_ref.at[onward]).start()
+
         to_each(lambda c: c.start())
-
-        @pl.when(group < n_groups - 1)
-        def _():
-            to_next(vector_ref.at[onward]).start()
-
         vector_ref[arrived] = vector_ref[entry]
 
-    @pl.when(both(jnp.logical_not(head), jnp.logical_not(origin)))
+    @pl.when(jnp.logical_and(tm > 0, jnp.logical_not(head)))
     def _():
         copy(
             vector_ref.at[entry], vector_ref.at[arrived], spread_send.at[0], vector_recv,
@@ -516,14 +588,20 @@
     n_tm, n_sub, n_inner = sizes
     steps, state = guess.shape
     rows = state + tail
+    hidden = layer_bias.shape[0]
     vmem = pl.BlockSpec(memory_space=pltpu.VMEM)
     dma, regular = pltpu.SemaphoreType.DMA, pltpu.SemaphoreType.REGULAR
     return pl.pallas_call(
         functools.partial(kernel, sizes),
-        out_shape=jax.ShapeDtypeStruct((steps, state), f32),
-        in_specs=[vmem] * 5,
+        out_shape=pltpu.VMEM((steps, state), f32),
+        in_specs=[pl.BlockSpec(memory_space=pl.ANY)] * 5,
         out_specs=vmem,
         scratch_shapes=[
+            pltpu.VMEM((steps, state), f32),
+            pltpu.VMEM((1, state), f32),
+            pltpu.VMEM((state // 2, hidden), f32),
+            pltpu.VMEM((1, hidden), f32),
+            pltpu.VMEM((1, hidden), f32),
             pltpu.VMEM((steps, 2 * state, 2 * state), bf16),
             pltpu.VMEM((2 * state, state), bf16),
             pltpu.VMEM((2, steps, state), f32),
@@ -536,6 +614,9 @@
             pltpu.VMEM((rows, state), f32),
             pltpu.VMEM((3 + planes, tail, state), f32),
             pltpu.VMEM((steps, rows, state), f32),
+            pltpu.VMEM((2 * state, hidden), bf16),
+            pltpu.VMEM((hidden, 2 * state), bf16),
+            pltpu.VMEM((steps, state), f32),
             dma((2,)),
             dma((n_sub,)),
             dma((n_sub,)),
@@ -546,6 +627,8 @@
             dma,
             dma,
             dma,
+            dma,
+            dma((5,)),
         ],
         compiler_params=pltpu.CompilerParams(collective_id=0, has_side_effects=True),
     )(guess, start.reshape(1, -1), layer_weight.T, layer_bias.reshape(1, -1), amplitude.reshape(1, -1))

time: 50.6 us -> 48.5 us (0.958)
  Pallas kernels: 49.1 us -> 47.7 us
  local copies, waits for them, and re-layouts: 1.3 us -> 0.6 us
    pallas_call x1, Pallas kernels: 49.1 us -> 47.7 us  [shards(): pl.pallas_call(functools.partial(kernel, sizes), out_shape=pltpu.VMEM((st...]
    unnamed x1, local copies, waits for them, and re-layouts: 1.3 us -> 0.6 us
where the time goes in v3:
time: 48.5 us; the launch traced here: 48.4 us
  Pallas kernels  47.7 us (98%)
  local copies, waits for them, and re-layouts  0.6 us (1%)
    pallas_call x1, Pallas kernels, shards(): pl.pallas_call(functools.partial(kernel, sizes), out_shape=pltpu.VMEM((st...  47.7 us

profile of v3, /device:TPU:33, one launch (start us, length us, event | category | flops | bytes accessed | tf_op | source)
XLA Modules:
  0.0 48.4 jit_solution(4759045999236672943)
XLA Ops:
  0.0 47.7 %shard_map.55 = f32[16,128]{1,0:T(8,128)S(1)} custom-call(f32[16,128]{1,0:T(8,128)} %guess_hbm.1, f32[1,128]{1,0:T(1,128)} %bitcast.7, f32[64,256]{1,0:T(8,128)} %bitcast.4, f32[1,256]{1,0:T(1,128)} %bitcast.5, f32[1,256]{1,0:T(1,128)} %bitcast.6), custom_call_target="tpu_custom_call" | custom-call | tf_op jit(solution)/shard_map/pallas_call | solution.py:594
  47.8 0.6 %copy.7 = f32[16,128]{1,0:T(8,128)} copy(f32[16,128]{1,0:T(8,128)S(1)} %shard_map.55) | data formatting | bytes 16384

commit v4 on v3

--- a/solution.py
+++ b/solution.py
@@ -80,11 +80,23 @@
     return (iota((rows, state), 0) == iota((rows, state), 1)).astype(f32)
 
 
-def applied(vector, full):
-    state = vector.shape[1]
-    eye = iota((state, state), 0) == iota((state, state), 1)
-    column = jnp.sum(jnp.where(eye, vector, 0.0), axis=1, keepdims=True)
+def diagonal_mask(state):
+    return iota((state, state), 0) == iota((state, state), 1)
+
+
+def stand(row):
+    return jnp.sum(jnp.where(diagonal_mask(row.shape[1]), row, 0.0), axis=1, keepdims=True)
+
+
+def laid(column, full):
+    state = full.shape[1]
     return jnp.sum(column * full[:state], axis=0, keepdims=True) + full[state : state + 1]
+
+
+def stood(row, full):
+    state = full.shape[1]
+    shift = jnp.where(diagonal_mask(state), full[state : state + 1], 0.0)
+    return jnp.sum(full[:state].T * row + shift, axis=1, keepdims=True)
 
 
 class Weights:
@@ -200,30 +212,33 @@
     return chain([join(*s) for s in states])
 
 
+def run_lengths(steps):
+    return [steps // 4] * 4
+
+
 def left_state(weights, rows, start):
     window = Window(weights, rows, start)
     steps, state = window.steps, window.state
     width = state // 2
-    runs = 4
-    length = steps // runs
-    hessians = weights.hessians(window.curves, window.diagonal)
+    lengths = run_lengths(steps)
+    begins = [sum(lengths[:c]) for c in range(len(lengths))]
+    hessians = weights.hessians(window.curves[:steps], window.diagonal)
     repeated = jnp.where(iota((width, state), 0) == iota((width, state), 1) % width, 1.0, 0.0)
     none = jnp.zeros((tail, state), f32)
     moving = jnp.concatenate([repeated, step_size * repeated, none], axis=0)
     states = [(window.begin_q, window.begin_p)]
-    for c in range(1, runs):
-        t = c * length
+    for t in begins[1:]:
         bend = half_step * hessians[t]
         momenta = jnp.concatenate([-bend, repeated - step_size * bend, none], axis=0)
         states.append((
             with_tail(moving, window.off_q[t : t + 1]),
             with_tail(momenta, window.off_p[t : t + 1]),
         ))
-    for j in range(length):
-        for c in range(runs):
-            if j == length - 1 and c > 0:
+    for j in range(max(lengths)):
+        for c, length in enumerate(lengths):
+            t = begins[c] + j + (1 if c else 0)
+            if t >= begins[c] + length:
                 continue
-            t = c * length + j + (1 if c else 0)
             coords, momenta = states[c]
             coords = coords + step_size * momenta
             momenta = momenta - kick(coords, stationary(hessians[t]))
@@ -232,10 +247,11 @@
                 with_tail(momenta, window.off_p[t : t + 1]),
             )
     maps = [join(*s) for s in states]
-    vector = maps[0][:1]
+    vector, upright = maps[0][:1], False
     for full in maps[1:]:
-        vector = applied(vector, full)
-    return vector
+        vector = laid(vector, full) if upright else stood(vector, full)
+        upright = not upright
+    return vector if upright else stand(vector)
 
 
 def kernel(
@@ -243,8 +259,8 @@
     guess_ref, start_ref, weight_ref, bias_ref, amplitude_ref,
     kicks_ref, open_ref, offs_ref, rows_ref, core_ref, subs_ref, majors_ref, ahead_ref,
     pre_ref, run_ref, vector_ref, maps_ref, onto_ref, back_ref, raw_ref,
-    core_sems, subs_send, subs_recv, majors_send, majors_recv, pre_sems,
-    spread_send, vector_recv, entry_send, entry_recv, raw_recv, load_sems,
+    upright_ref, pair_send, pair_recv, subs_send, subs_recv, column_send, majors_recv,
+    spread_send, state_recv, load_guess, load_last,
 ):
     n_tm, n_sub, n_inner = sizes
     n_groups = n_tm // planes
@@ -280,30 +296,29 @@
     barrier = pltpu.get_barrier_semaphore()
     around = n_sub * n_inner
     loads = [
-        pltpu.make_async_copy(source, target, load_sems.at[k])
-        for k, (source, target) in enumerate((
-            (guess_hbm, guess_ref), (weight_hbm, weight_ref), (start_hbm, start_ref),
-            (bias_hbm, bias_ref), (amplitude_hbm, amplitude_ref),
-        ))
+        pltpu.make_async_copy(source, target, sem)
+        for source, target, sem in (
+            (guess_hbm, guess_ref, load_guess), (weight_hbm, weight_ref, subs_send),
+            (start_hbm, start_ref, column_send), (bias_hbm, bias_ref, pair_send),
+            (amplitude_hbm, amplitude_ref, load_last),
+        )
     ]
-    for load in loads:
-        load.start()
-
-    def from_origin(act):
-        def send(at, carry):
-            act(copy(
-                guess_ref, raw_ref, spread_send.at[at], raw_recv,
-                place(0, lax.div(at, n_inner), lax.rem(at, n_inner)),
-            ))
-            return carry
-
-        lax.fori_loop(1, around, send, 0)
+    loads[0].start()
+
+    def from_origin(at):
+        return copy(
+            guess_ref, raw_ref, spread_send, state_recv, place(0, at // n_inner, at % n_inner)
+        )
 
     @pl.when(origin)
     def _():
         pl.semaphore_wait(barrier, around - 1)
         loads[0].wait()
-        from_origin(lambda c: c.start())
+        for at in range(1, around):
+            from_origin(at).start()
+
+    for load in loads[1:]:
+        load.start()
 
     @pl.when(jnp.logical_not(origin))
     def _():
@@ -322,9 +337,13 @@
         def _():
             greet(place(0, 0, 0))
 
-        @pl.when(both(tm > 0, jnp.logical_not(head)))
-        def _():
-            greet(place(group * planes, 0, last))
+        @pl.when(both(tm > 0, jnp.logical_not(column)))
+        def _():
+            greet(place(tm, 0, last))
+
+        @pl.when(both(column, plane > 0))
+        def _():
+            greet(place(group * planes))
 
     def takes_from(s):
         return both(lead, sub != s, jnp.logical_or(sub > s, sub == 0))
@@ -360,8 +379,8 @@
     count = count + jnp.where(other, 1, 0)
     count = count + jnp.where(lead, jnp.where(sub == 0, n_sub - 1, n_sub - sub), 0)
     count = count + jnp.where(jnp.logical_and(column, plane > 0), 1, 0)
-    count = count + jnp.where(head, (planes - 1) * around, 0)
-    count = count + jnp.where(jnp.logical_and(head, group > 0), around - 1, 0)
+    count = count + jnp.where(head, planes - 1, 0)
+    count = count + jnp.where(jnp.logical_and(column, tm > 0), around - 1, 0)
     count = count + jnp.where(jnp.logical_and(head, group < n_groups - 1), 1, 0)
 
     @pl.when(jnp.logical_not(origin))
@@ -369,11 +388,10 @@
         pl.semaphore_wait(barrier, count)
 
     entry, arrived, onward = 0, planes + 1, planes + 2
-    entering = vector_ref.at[entry]
 
     @pl.when(origin)
     def _():
-        vector_ref[arrived] = jnp.broadcast_to(window.first, (tail, state))
+        upright_ref[...] = jnp.broadcast_to(stand(window.first), (state, state))
 
     for t in range(steps):
         kicks_ref[t, :, :state] = found[t]
@@ -386,18 +404,24 @@
     for t in range(steps):
         kicks_ref[t, :, state:] = stationary(plain[t])
 
-    to_lead = copy(run_ref, core_ref, core_sems.at[0], core_sems.at[1], place(inner_at=last))
-    to_other = copy(pre_ref, pre_ref, pre_sems.at[0], pre_sems.at[1], place(inner_at=0))
+    to_lead = copy(run_ref, core_ref, pair_send, pair_recv, place(inner_at=last))
+    to_other = copy(pre_ref, pre_ref, pair_send, pair_recv, place(inner_at=0))
     to_head = copy(
-        majors_ref.at[plane], majors_ref.at[plane], majors_send, majors_recv.at[plane],
+        majors_ref.at[plane], majors_ref.at[plane], column_send, majors_recv,
         place(group * planes),
     )
 
     def to_sub(t):
         return copy(
-            subs_ref.at[sub], subs_ref.at[sub], subs_send.at[t], subs_recv.at[sub],
-            place(sub_at=t),
-        )
+            subs_ref.at[sub], subs_ref.at[sub], subs_send, subs_recv, place(sub_at=t)
+        )
+
+    def some_subs(count):
+        part_of = subs_ref.at[pl.ds(0, count)]
+        return copy(part_of, part_of, subs_send, subs_recv, place())
+
+    given = jnp.where(sub == 0, n_sub - 1, n_sub - sub)
+    taken = jnp.where(sub == 0, n_sub - 1, sub)
 
     @pl.when(jnp.logical_and(other, jnp.logical_not(origin)))
     def _():
@@ -419,13 +443,10 @@
             def _():
                 to_sub(t).start()
 
-        for s in range(n_sub):
-            @pl.when(takes_from(s))
+        for k in range(1, n_sub):
+            @pl.when(taken == k)
             def _():
-                copy(
-                    subs_ref.at[s], subs_ref.at[s], subs_send.at[s], subs_recv.at[s],
-                    place(sub_at=s),
-                ).wait_recv()
+                some_subs(k).wait_recv()
 
         pre_ref[...] = identity(state)
         for k in range(n_sub - 1):
@@ -453,11 +474,9 @@
             @pl.when(plane == 0)
             def _():
                 ahead_ref[0] = majors_ref[0]
+                others = majors_ref.at[pl.ds(1, planes - 1)]
+                copy(others, others, column_send, majors_recv, place()).wait_recv()
                 for k in range(1, planes):
-                    copy(
-                        majors_ref.at[k], majors_ref.at[k], majors_send, majors_recv.at[k],
-                        place(group * planes + k),
-                    ).wait_recv()
                     ahead_ref[k] = compose(ahead_ref[k - 1], majors_ref[k])
 
     @pl.when(other)
@@ -492,80 +511,88 @@
 
     lax.fori_loop(0, steps - 1, advance, (coords, momenta))
 
-    def to_next(source):
-        return copy(source, entering, entry_send, entry_recv, place((group + 1) * planes))
-
-    def to_each(act):
-        def send(at, carry):
-            @pl.when(at != last)
-            def _():
-                k = lax.div(at, around)
-                act(copy(
-                    vector_ref.at[k], vector_ref.at[arrived], spread_send.at[at], vector_recv,
-                    place(
-                        group * planes + k,
-                        lax.rem(lax.div(at, n_inner), n_sub),
-                        lax.rem(at, n_inner),
-                    ),
-                ))
-
-            return carry
-
-        lax.fori_loop(jnp.where(group > 0, 0, around), planes * around, send, 0)
-
-    late = jnp.logical_and(tm == 0, jnp.logical_not(origin))
-
-    @pl.when(late)
-    def _():
-        copy(guess_ref, raw_ref, spread_send.at[0], raw_recv, place(0, 0, 0)).wait_recv()
-        left = jnp.broadcast_to(left_state(weights, raw_ref[...], start_ref[...]), (tail, state))
-        vector_ref[entry] = left
-        vector_ref[arrived] = left
+    to_next = copy(
+        vector_ref.at[onward], vector_ref.at[entry], column_send, state_recv,
+        place((group + 1) * planes),
+    )
+
+    def to_plane(k):
+        return copy(
+            vector_ref.at[k], vector_ref.at[arrived], spread_send, state_recv,
+            place(group * planes + k),
+        )
+
+    def to_device(at):
+        return copy(
+            vector_ref.at[arrived], vector_ref.at[arrived], spread_send, state_recv,
+            place(tm, at // n_inner, at % n_inner),
+        )
+
+    def spread():
+        for at in range(around):
+            if at != last:
+                to_device(at).start()
+
+    def stand_at(slot):
+        upright_ref[...] = jnp.broadcast_to(stand(vector_ref[slot]), (state, state))
+
+    @pl.when(jnp.logical_and(tm == 0, jnp.logical_not(origin)))
+    def _():
+        copy(guess_ref, raw_ref, spread_send, state_recv, place(0, 0, 0)).wait_recv()
+        left = left_state(weights, raw_ref[...], start_ref[...])
+        upright_ref[...] = jnp.broadcast_to(left, (state, state))
 
     @pl.when(head)
     def _():
         @pl.when(group > 0)
         def _():
-            to_next(vector_ref.at[onward]).wait_recv()
-
-        here = vector_ref[entry, :1, :]
+            to_next.wait_recv()
+            stand_at(entry)
+
         for k in range(planes):
-            slot = k + 1 if k + 1 < planes else onward
-            vector_ref[slot] = jnp.broadcast_to(applied(here, ahead_ref[k]), (tail, state))
+            vector_ref[k + 1 if k + 1 < planes else onward] = laid(upright_ref[...], ahead_ref[k])
 
         @pl.when(group < n_groups - 1)
         def _():
-            to_next(vector_ref.at[onward]).start()
-
-        to_each(lambda c: c.start())
-        vector_ref[arrived] = vector_ref[entry]
+            to_next.start()
+
+        for k in range(1, planes):
+            to_plane(k).start()
+
+        @pl.when(group > 0)
+        def _():
+            vector_ref[arrived] = vector_ref[entry]
+            spread()
 
     @pl.when(jnp.logical_and(tm > 0, jnp.logical_not(head)))
     def _():
-        copy(
-            vector_ref.at[entry], vector_ref.at[arrived], spread_send.at[0], vector_recv,
-            place(group * planes, 0, last),
-        ).wait_recv()
-
-    vector = vector_ref[arrived, :1, :]
-    eye = iota((state, state), 0) == iota((state, state), 1)
-    upright = jnp.sum(jnp.where(eye, vector, 0.0), axis=1, keepdims=True)
+        to_device(0).wait_recv()
+
+        @pl.when(column)
+        def _():
+            spread()
+
+        stand_at(arrived)
+
+    upright = upright_ref[...]
     for t in range(steps):
         ref = run_ref if t == 0 else maps_ref.at[t - 1]
-        out_ref[t : t + 1, :] = (
-            jnp.sum(upright * ref[:state, :], axis=0, keepdims=True) + ref[state : state + 1, :]
-        )
+        out_ref[t : t + 1, :] = laid(upright, ref)
+
+    def spread_left(rows):
+        sent = maps_ref.at[0, pl.ds(0, rows), :]
+        copy(sent, sent, spread_send, state_recv, place()).wait_send()
 
     @pl.when(origin)
     def _():
-        from_origin(lambda c: c.wait_send())
+        spread_left((around - 1) * steps)
 
     @pl.when(lead)
     def _():
-        for t in range(n_sub):
-            @pl.when(gives_to(t))
+        for k in range(1, n_sub):
+            @pl.when(given == k)
             def _():
-                to_sub(t).wait_send()
+                some_subs(k).wait_send()
 
         @pl.when(jnp.logical_not(opening_chip))
         def _():
@@ -575,13 +602,25 @@
         def _():
             to_head.wait_send()
 
-    @pl.when(head)
-    def _():
-        to_each(lambda c: c.wait_send())
-
-        @pl.when(group < n_groups - 1)
-        def _():
-            to_next(vector_ref.at[onward]).wait_send()
+    @pl.when(column)
+    def _():
+        ahead = planes - 1
+
+        @pl.when(both(head, tm > 0))
+        def _():
+            spread_left(ahead + around - 1)
+
+        @pl.when(both(head, tm == 0))
+        def _():
+            spread_left(ahead)
+
+        @pl.when(plane > 0)
+        def _():
+            spread_left(around - 1)
+
+    @pl.when(both(head, group < n_groups - 1))
+    def _():
+        to_next.wait_send()
 
 
 def shards(sizes, guess, start, layer_weight, layer_bias, amplitude):
@@ -590,7 +629,7 @@
     rows = state + tail
     hidden = layer_bias.shape[0]
     vmem = pl.BlockSpec(memory_space=pltpu.VMEM)
-    dma, regular = pltpu.SemaphoreType.DMA, pltpu.SemaphoreType.REGULAR
+    dma = pltpu.SemaphoreType.DMA
     return pl.pallas_call(
         functools.partial(kernel, sizes),
         out_shape=pltpu.VMEM((steps, state), f32),
@@ -612,23 +651,22 @@
             pltpu.VMEM((planes, rows, state), f32),
             pltpu.VMEM((rows, state), f32),
             pltpu.VMEM((rows, state), f32),
-            pltpu.VMEM((3 + planes, tail, state), f32),
+            pltpu.VMEM((3 + planes, 1, state), f32),
             pltpu.VMEM((steps, rows, state), f32),
             pltpu.VMEM((2 * state, hidden), bf16),
             pltpu.VMEM((hidden, 2 * state), bf16),
             pltpu.VMEM((steps, state), f32),
-            dma((2,)),
-            dma((n_sub,)),
-            dma((n_sub,)),
-            dma,
-            dma((planes,)),
-            dma((2,)),
-            dma((planes * n_sub * n_inner,)),
-            dma,
-            dma,
-            dma,
-            dma,
-            dma((5,)),
+            pltpu.VMEM((state, state), f32),
+            dma,
+            dma,
+            dma,
+            dma,
+            dma,
+            dma,
+            dma,
+            dma,
+            dma,
+            dma,
         ],
         compiler_params=pltpu.CompilerParams(collective_id=0, has_side_effects=True),
     )(guess, start.reshape(1, -1), layer_weight.T, layer_bias.reshape(1, -1), amplitude.reshape(1, -1))

time: 48.5 us -> 47.1 us (0.971)
  Pallas kernels: 47.7 us -> 46.3 us
    pallas_call x1, Pallas kernels: 47.7 us -> 46.3 us  [shards(): pl.pallas_call(functools.partial(kernel, sizes), out_shape=pltpu.VMEM((st...]
where the time goes in v4:
time: 47.1 us; the launch traced here: 46.9 us
  Pallas kernels  46.3 us (98%)
  local copies, waits for them, and re-layouts  0.6 us (1%)
    pallas_call x1, Pallas kernels, shards(): pl.pallas_call(functools.partial(kernel, sizes), out_shape=pltpu.VMEM((st...  46.3 us

profile of v4, /device:TPU:33, one launch (start us, length us, event | category | flops | bytes accessed | tf_op | source)
XLA Modules:
  0.0 46.9 jit_solution(4179309518253329174)
XLA Ops:
  0.0 46.3 %shard_map.55 = f32[16,128]{1,0:T(8,128)S(1)} custom-call(f32[16,128]{1,0:T(8,128)} %guess_hbm.1, f32[1,128]{1,0:T(1,128)} %bitcast.7, f32[64,256]{1,0:T(8,128)} %bitcast.4, f32[1,256]{1,0:T(1,128)} %bitcast.5, f32[1,256]{1,0:T(1,128)} %bitcast.6), custom_call_target="tpu_custom_call" | custom-call | tf_op jit(solution)/shard_map/pallas_call | solution.py:633
  46.3 0.6 %copy.7 = f32[16,128]{1,0:T(8,128)} copy(f32[16,128]{1,0:T(8,128)S(1)} %shard_map.55) | data formatting | bytes 16384

commit v5 on v4

--- a/solution.py
+++ b/solution.py
@@ -13,6 +13,7 @@
 f32, bf16 = jnp.float32, jnp.bfloat16
 MESH = pl.DeviceIdType.MESH
 planes = 4
+home = 1
 tail = 8
 
 
@@ -272,9 +273,12 @@
     lead = inner == last
     other = jnp.logical_not(lead)
     column = jnp.logical_and(lead, sub == 0)
-    head = jnp.logical_and(column, plane == 0)
+    head = jnp.logical_and(column, plane == home)
     opening_chip = jnp.logical_and(tm == 0, sub == 0)
     origin = jnp.logical_and(opening_chip, inner == 0)
+    starts = jnp.logical_and(
+        jnp.logical_not(origin), jnp.logical_or(tm == 0, jnp.logical_and(head, group == 0))
+    )
 
     def place(tm_at=None, sub_at=None, inner_at=None):
         return (
@@ -306,15 +310,14 @@
     loads[0].start()
 
     def from_origin(at):
-        return copy(
-            guess_ref, raw_ref, spread_send, state_recv, place(0, at // n_inner, at % n_inner)
-        )
+        where = place(0, at // n_inner, at % n_inner) if at < around else place(home, 0, last)
+        return copy(guess_ref, raw_ref, spread_send, state_recv, where)
 
     @pl.when(origin)
     def _():
-        pl.semaphore_wait(barrier, around - 1)
+        pl.semaphore_wait(barrier, around)
         loads[0].wait()
-        for at in range(1, around):
+        for at in range(1, around + 1):
             from_origin(at).start()
 
     for load in loads[1:]:
@@ -333,7 +336,7 @@
         def _():
             greet(place(inner_at=n_inner - 1 - inner))
 
-        @pl.when(tm == 0)
+        @pl.when(starts)
         def _():
             greet(place(0, 0, 0))
 
@@ -341,9 +344,9 @@
         def _():
             greet(place(tm, 0, last))
 
-        @pl.when(both(column, plane > 0))
-        def _():
-            greet(place(group * planes))
+        @pl.when(both(column, tm > 0, plane != home))
+        def _():
+            greet(place(group * planes + home))
 
     def takes_from(s):
         return both(lead, sub != s, jnp.logical_or(sub > s, sub == 0))
@@ -358,12 +361,13 @@
 
     @pl.when(head)
     def _():
-        for k in range(1, planes):
-            greet(place(group * planes + k))
+        for k in range(planes):
+            if k != home:
+                greet(place(group * planes + k))
 
         @pl.when(group > 0)
         def _():
-            greet(place((group - 1) * planes))
+            greet(place((group - 1) * planes + home))
 
     for load in loads[1:]:
         load.wait()
@@ -378,8 +382,8 @@
     count = jnp.where(jnp.logical_and(lead, jnp.logical_not(opening_chip)), 1, 0)
     count = count + jnp.where(other, 1, 0)
     count = count + jnp.where(lead, jnp.where(sub == 0, n_sub - 1, n_sub - sub), 0)
-    count = count + jnp.where(jnp.logical_and(column, plane > 0), 1, 0)
-    count = count + jnp.where(head, planes - 1, 0)
+    count = count + jnp.where(jnp.logical_and(column, plane != home), 1, 0)
+    count = count + jnp.where(head, jnp.where(group > 0, planes - 1, planes - 2), 0)
     count = count + jnp.where(jnp.logical_and(column, tm > 0), around - 1, 0)
     count = count + jnp.where(jnp.logical_and(head, group < n_groups - 1), 1, 0)
 
@@ -408,7 +412,7 @@
     to_other = copy(pre_ref, pre_ref, pair_send, pair_recv, place(inner_at=0))
     to_head = copy(
         majors_ref.at[plane], majors_ref.at[plane], column_send, majors_recv,
-        place(group * planes),
+        place(group * planes + home),
     )
 
     def to_sub(t):
@@ -467,15 +471,15 @@
         def _():
             majors_ref[plane] = chain([subs_ref[k] for k in range(n_sub)])
 
-            @pl.when(plane > 0)
+            @pl.when(plane != home)
             def _():
                 to_head.start()
 
-            @pl.when(plane == 0)
+            @pl.when(plane == home)
             def _():
+                others = majors_ref.at[pl.ds(0, planes - 1)]
+                copy(others, others, column_send, majors_recv, place()).wait_recv()
                 ahead_ref[0] = majors_ref[0]
-                others = majors_ref.at[pl.ds(1, planes - 1)]
-                copy(others, others, column_send, majors_recv, place()).wait_recv()
                 for k in range(1, planes):
                     ahead_ref[k] = compose(ahead_ref[k - 1], majors_ref[k])
 
@@ -513,7 +517,7 @@
 
     to_next = copy(
         vector_ref.at[onward], vector_ref.at[entry], column_send, state_recv,
-        place((group + 1) * planes),
+        place((group + 1) * planes + home),
     )
 
     def to_plane(k):
@@ -536,7 +540,7 @@
     def stand_at(slot):
         upright_ref[...] = jnp.broadcast_to(stand(vector_ref[slot]), (state, state))
 
-    @pl.when(jnp.logical_and(tm == 0, jnp.logical_not(origin)))
+    @pl.when(starts)
     def _():
         copy(guess_ref, raw_ref, spread_send, state_recv, place(0, 0, 0)).wait_recv()
         left = left_state(weights, raw_ref[...], start_ref[...])
@@ -550,21 +554,25 @@
             stand_at(entry)
 
         for k in range(planes):
-            vector_ref[k + 1 if k + 1 < planes else onward] = laid(upright_ref[...], ahead_ref[k])
+            slot = k + 1 if k + 1 < planes else onward
+            vector_ref[arrived if slot == home else slot] = laid(upright_ref[...], ahead_ref[k])
 
         @pl.when(group < n_groups - 1)
         def _():
             to_next.start()
 
         for k in range(1, planes):
-            to_plane(k).start()
+            if k != home:
+                to_plane(k).start()
 
         @pl.when(group > 0)
         def _():
-            vector_ref[arrived] = vector_ref[entry]
-            spread()
-
-    @pl.when(jnp.logical_and(tm > 0, jnp.logical_not(head)))
+            to_plane(0).start()
+
+        spread()
+        stand_at(arrived)
+
+    @pl.when(both(tm > 0, jnp.logical_not(head)))
     def _():
         to_device(0).wait_recv()
 
@@ -585,7 +593,7 @@
 
     @pl.when(origin)
     def _():
-        spread_left((around - 1) * steps)
+        spread_left(around * steps)
 
     @pl.when(lead)
     def _():
@@ -598,25 +606,21 @@
         def _():
             to_other.wait_send()
 
-        @pl.when(jnp.logical_and(column, plane > 0))
+        @pl.when(jnp.logical_and(column, plane != home))
         def _():
             to_head.wait_send()
 
-    @pl.when(column)
-    def _():
-        ahead = planes - 1
-
-        @pl.when(both(head, tm > 0))
-        def _():
-            spread_left(ahead + around - 1)
-
-        @pl.when(both(head, tm == 0))
-        def _():
-            spread_left(ahead)
-
-        @pl.when(plane > 0)
-        def _():
-            spread_left(around - 1)
+    @pl.when(both(head, group > 0))
+    def _():
+        spread_left(planes + around - 2)
+
+    @pl.when(both(head, group == 0))
+    def _():
+        spread_left(planes + around - 3)
+
+    @pl.when(both(column, tm > 0, plane != home))
+    def _():
+        spread_left(around - 1)
 
     @pl.when(both(head, group < n_groups - 1))
     def _():

time: 47.1 us -> 46.5 us (0.987)
  Pallas kernels: 46.3 us -> 45.6 us
    pallas_call x1, Pallas kernels: 46.3 us -> 45.6 us  [shards(): pl.pallas_call(functools.partial(kernel, sizes), out_shape=pltpu.VMEM((st...]
where the time goes in v5:
time: 46.5 us; the launch traced here: 46.2 us
  Pallas kernels  45.6 us (98%)
  local copies, waits for them, and re-layouts  0.6 us (1%)
    pallas_call x1, Pallas kernels, shards(): pl.pallas_call(functools.partial(kernel, sizes), out_shape=pltpu.VMEM((st...  45.6 us

profile of v5, /device:TPU:33, one launch (start us, length us, event | category | flops | bytes accessed | tf_op | source)
XLA Modules:
  0.0 46.2 jit_solution(1999091743513715704)
XLA Ops:
  0.0 45.6 %shard_map.55 = f32[16,128]{1,0:T(8,128)S(1)} custom-call(f32[16,128]{1,0:T(8,128)} %guess_hbm.1, f32[1,128]{1,0:T(1,128)} %bitcast.7, f32[64,256]{1,0:T(8,128)} %bitcast.4, f32[1,256]{1,0:T(1,128)} %bitcast.5, f32[1,256]{1,0:T(1,128)} %bitcast.6), custom_call_target="tpu_custom_call" | custom-call | tf_op jit(solution)/shard_map/pallas_call | solution.py:637
  45.6 0.6 %copy.7 = f32[16,128]{1,0:T(8,128)} copy(f32[16,128]{1,0:T(8,128)S(1)} %shard_map.55) | data formatting | bytes 16384

commit v6 on v5

--- a/solution.py
+++ b/solution.py
@@ -118,9 +118,9 @@
 
     def apart(self, value):
         back = self.back_ref[...]
-        state = back.shape[1] // 2
-        high, low = split(value)
-        out = dot(high, back) + dot(low, back)
+        state, rows = back.shape[1] // 2, value.shape[0]
+        out = dot(jnp.concatenate(split(value), axis=0), back)
+        out = out[:rows] + out[rows:]
         return out[:, :state] + out[:, state:]
 
     def forces(self, coords):
@@ -214,7 +214,9 @@
 
 
 def run_lengths(steps):
-    return [steps // 4] * 4
+    short = steps // 8
+    found = [short, short] + [(steps - 2 * short) // 4] * 4
+    return found[:-1] + [steps - sum(found[:-1])]
 
 
 def left_state(weights, rows, start):

time: 46.5 us -> 46.3 us (level)
  no operation moved by 1% of the time
where the time goes in v6:
time: 46.3 us; the launch traced here: 46 us
  Pallas kernels  45.3 us (98%)
  local copies, waits for them, and re-layouts  0.6 us (1%)
    pallas_call x1, Pallas kernels, shards(): pl.pallas_call(functools.partial(kernel, sizes), out_shape=pltpu.VMEM((st...  45.3 us

profile of v6, /device:TPU:33, one launch (start us, length us, event | category | flops | bytes accessed | tf_op | source)
XLA Modules:
  0.0 46.0 jit_solution(5651170989957994874)
XLA Ops:
  0.0 45.3 %shard_map.55 = f32[16,128]{1,0:T(8,128)S(1)} custom-call(f32[16,128]{1,0:T(8,128)} %guess_hbm.1, f32[1,128]{1,0:T(1,128)} %bitcast.7, f32[64,256]{1,0:T(8,128)} %bitcast.4, f32[1,256]{1,0:T(1,128)} %bitcast.5, f32[1,256]{1,0:T(1,128)} %bitcast.6), custom_call_target="tpu_custom_call" | custom-call | tf_op jit(solution)/shard_map/pallas_call | solution.py:639
  45.4 0.6 %copy.7 = f32[16,128]{1,0:T(8,128)} copy(f32[16,128]{1,0:T(8,128)S(1)} %shard_map.55) | data formatting | bytes 16384

commit v7 on v6

--- a/solution.py
+++ b/solution.py
@@ -26,6 +26,11 @@
     return high, (value - high.astype(f32)).astype(bf16)
 
 
+def thirds(value):
+    high, rest = value.astype(bf16), value - value.astype(bf16).astype(f32)
+    return (high, *split(rest))
+
+
 def low_lanes(value):
     width = value.shape[-1]
     return iota(value.shape, 1) < width // 2
@@ -60,11 +65,14 @@
 def compose(first, second):
     state = first.shape[1]
     eye = (iota((state, state), 0) == iota((state, state), 1)).astype(f32)
-    high, low = split(second[:state] - eye)
-    both = jnp.concatenate([high, low], axis=1)
-    left = jnp.concatenate(split(first), axis=1)
+    high, middle, low = thirds(second[:state] - eye)
+    both = jnp.concatenate([high, middle], axis=1)
+    high_left, middle_left, low_left = thirds(first)
+    left = jnp.concatenate([high_left, middle_left], axis=1)
     out = dot(left, jnp.concatenate([both, both], axis=0))
-    return with_tail(first + (out[:, :state] + out[:, state:]), second[state:])
+    left = jnp.concatenate([high_left, low_left], axis=1)
+    small = dot(left, jnp.concatenate([low, high], axis=0))
+    return with_tail(first + (out[:, :state] + (out[:, state:] + small)), second[state:])
 
 
 def chain(maps):

time: 46.3 us -> 46.3 us (level)
  no operation moved by 1% of the time
where the time goes in v7:
time: 46.3 us; the launch traced here: 46 us
  Pallas kernels  45.3 us (98%)
  local copies, waits for them, and re-layouts  0.6 us (1%)
    pallas_call x1, Pallas kernels, shards(): pl.pallas_call(functools.partial(kernel, sizes), out_shape=pltpu.VMEM((st...  45.3 us

profile of v7, /device:TPU:33, one launch (start us, length us, event | category | flops | bytes accessed | tf_op | source)
XLA Modules:
  0.0 46.0 jit_solution(962048442951251691)
XLA Ops:
  0.0 45.3 %shard_map.55 = f32[16,128]{1,0:T(8,128)S(1)} custom-call(f32[16,128]{1,0:T(8,128)} %guess_hbm.1, f32[1,128]{1,0:T(1,128)} %bitcast.7, f32[64,256]{1,0:T(8,128)} %bitcast.4, f32[1,256]{1,0:T(1,128)} %bitcast.5, f32[1,256]{1,0:T(1,128)} %bitcast.6), custom_call_target="tpu_custom_call" | custom-call | tf_op jit(solution)/shard_map/pallas_call | solution.py:647
  45.4 0.6 %copy.7 = f32[16,128]{1,0:T(8,128)} copy(f32[16,128]{1,0:T(8,128)S(1)} %shard_map.55) | data formatting | bytes 16384
